TPU v7x, 256 devices: a whole 4x4x8 slice. The times are simulated.
256 devices in a mesh: orb: 4 (over y), grid: 64 (over z, x, core).
Axes of the slice: x: 4, y: 4, z: 8, core: 2. Of those that a mesh axis runs over, the one named last changes fastest.
Arguments:
- orbitals: float32 [256, 2048, 128], P('orb', 'grid'), may hold values from -6 to 6
- previous: float32 [256, 2048, 128], P('orb', 'grid'), may hold values from -6 to 6
- potential: float32 [256, 2048, 128], P('orb', 'grid'), may hold values from -3 to 3
- partners: int32 [256, 3], P(('orb', 'grid')), may hold values from 0 to 255, as said below
- offsets: int32 [256, 3, 3], P(('orb', 'grid')), may hold values from -16 to 16, as said below
Outputs:
- advanced: float32 [256, 2048, 128], P('orb', 'grid')
- exchange_force: float32 [256, 2048, 128], P('orb', 'grid')
Inputs may be any that keep to these rules, and one draw needn't show every extreme that they name: `partners`: row n names three different orbitals among n + 1 to n + 4, counted modulo 256; so every intersecting pair is listed once, by its first orbital. There are integer box corners of the orbitals with offsets[n, q, :] = corner[partners[n, q]] - corner[n]; both ends of the range occur in every draw.
All inputs are finite; a program needn't handle non-finite values.
Results may differ from a plain program's by a relative error of at most 0.0003.
Values sent between devices are 32-bit elements; how exact they have to be, the bound alone decides.
No kernel may reach another device: no remote copies, remote signals or barrier semaphores. Data moves between devices by JAX's collectives and lax.ppermute only.
A program may use at most 128 MiB of HBM per device.

v0:
```python
import math

import jax
import jax.numpy as jnp
from jax import lax
from jax.sharding import Mesh
from jax.sharding import PartitionSpec as P

B = 64
SWEEPS = 4
AHEAD = 4
GRID = ("grid_0", "grid_1", "grid_2")
ORB_GRID = ("orb", "grid_0", "grid_1", "grid_2")


coulomb_factor = 4.0 * math.pi
exact_share = 0.25
verlet_factor = 0.05
lower_edge = 0.5
upper_edge = 16.0


def from_behind(array, axis, by):
    count = lax.axis_size(axis)
    return lax.ppermute(array, axis, [(i, (i + by) % count) for i in range(count)])


def cut_along(array, dim, count):
    before, after = (array.shape[:dim], array.shape[dim + 1 :])
    return jnp.moveaxis(array.reshape(*before, count, -1, *after), dim, 0)


def joined_along(blocks, dim):
    blocks = jnp.moveaxis(blocks, 0, dim)
    lengths = blocks.shape
    return blocks.reshape(*lengths[:dim], lengths[dim] * lengths[dim + 1], *lengths[dim + 2 :])


def exchange_in_order(blocks, axes, sequence):
    inside = blocks.shape[1:]
    out = blocks.reshape(*(lax.axis_size(a) for a in axes), *inside)
    for k in sequence:
        out = lax.all_to_all(out, axes[k], k, k, tiled=True)
    return out.reshape(-1, *inside)


def two_step_exchange(array, groups, sequence, split_dim, concat_dim):
    count = lax.axis_size(groups[0]) * lax.axis_size(groups[1])
    blocks = cut_along(array, split_dim, count)
    return joined_along(exchange_in_order(blocks, groups, sequence), concat_dim)


def apply_operator(grid_field):
    leading = grid_field.ndim - 3
    padded = jnp.pad(grid_field, [(0, 0)] * leading + [(2, 2)] * 3)
    extent = grid_field.shape[-1]

    def displaced(axis_number, offset_cells):
        corner = [2, 2, 2]
        corner[axis_number] = 2 + offset_cells
        return padded[
            ...,
            corner[0] : corner[0] + extent,
            corner[1] : corner[1] + extent,
            corner[2] : corner[2] + extent,
        ]

    nearest = (
        displaced(0, 1)
        + displaced(0, -1)
        + displaced(1, 1)
        + displaced(1, -1)
        + displaced(2, 1)
        + displaced(2, -1)
    )
    farther = (
        displaced(0, 2)
        + displaced(0, -2)
        + displaced(1, 2)
        + displaced(1, -2)
        + displaced(2, 2)
        + displaced(2, -2)
    )
    return 7.5 * grid_field - 4.0 / 3.0 * nearest + 1.0 / 12.0 * farther


def sweep_weights():
    centre = 0.5 * (upper_edge + lower_edge)
    radius = 0.5 * (upper_edge - lower_edge)
    ratio_sigma = centre / radius
    previous_rho = 1.0 / ratio_sigma
    weights = []
    for turn_index in range(SWEEPS - 1):
        current_rho = 1.0 / (2.0 * ratio_sigma - previous_rho)
        weights.append((current_rho * previous_rho, 2.0 * current_rho / radius))
        previous_rho = current_rho
    return (centre, weights)


def solve_potential(density):
    centre, weights = sweep_weights()
    residual = coulomb_factor * density
    direction = residual / centre
    solution = jnp.zeros_like(density)
    for turn_index in range(SWEEPS):
        solution = solution + direction
        residual = residual - apply_operator(direction)
        if turn_index + 1 < SWEEPS:
            keep_weight, residual_weight = weights[turn_index]
            direction = keep_weight * direction + residual_weight * residual
    return solution


def shift_box(one_box, offset, direction_sign):
    extent = one_box.shape[0]
    reach_cells = extent // 4
    padded = jnp.pad(one_box, reach_cells)
    corner = (reach_cells + direction_sign * offset).astype(jnp.int32)
    return lax.dynamic_slice(padded, (corner[0], corner[1], corner[2]), (extent, extent, extent))


def pair_terms(own_box, partner_boxes, pair_offsets):

    def single(partner_box, offset):
        moved_box = shift_box(partner_box, offset, 1)
        potential_box = solve_potential(own_box * moved_box)
        return (potential_box * moved_box, shift_box(potential_box * own_box, offset, -1))

    own_terms, partner_terms = jax.vmap(single)(partner_boxes, pair_offsets)
    return (jnp.sum(own_terms, axis=0), partner_terms)


def build_windows(orbitals, upper_rows, count_local, steps_ahead):
    slab_count = lax.axis_size(GRID)
    tail_shape = orbitals.shape[1:]
    blocks = jnp.concatenate([orbitals, upper_rows], axis=0)
    blocks = blocks.reshape((slab_count + steps_ahead, count_local) + tail_shape)
    ahead_rows = jnp.concatenate(
        [blocks[distance + 1 : distance + 1 + slab_count] for distance in range(steps_ahead)],
        axis=1,
    )
    windows = jnp.concatenate([blocks[:slab_count], ahead_rows], axis=1)
    return windows.reshape((slab_count * (count_local + AHEAD),) + tail_shape)


def fold_windows(returned, count_local, steps_ahead):
    slab_count = lax.axis_size(GRID)
    tail_shape = returned.shape[1:]
    blocks = returned.reshape((slab_count, count_local + AHEAD) + tail_shape)
    ahead_rows = blocks[:, count_local:]
    summed = jnp.pad(blocks[:, :count_local], ((0, steps_ahead), (0, 0), (0, 0), (0, 0)))
    for distance in range(steps_ahead):
        ahead_part = ahead_rows[:, distance * count_local : (distance + 1) * count_local]
        summed = summed + jnp.pad(
            ahead_part, ((distance + 1, steps_ahead - distance - 1), (0, 0), (0, 0), (0, 0))
        )
    flattened = summed.reshape(((slab_count + steps_ahead) * count_local,) + tail_shape)
    kept_rows = slab_count * count_local
    spilled = from_behind(flattened[kept_rows : kept_rows + AHEAD], "orb", 1)
    return flattened[:kept_rows] + jnp.pad(spilled, ((0, kept_rows - AHEAD), (0, 0), (0, 0)))


def local(orbitals, previous, potential, partners, offsets):
    count_local = partners.shape[0]
    width_last = orbitals.shape[2]
    total_orbitals = lax.axis_size(ORB_GRID) * count_local
    steps_ahead = -(-AHEAD // count_local)
    upper_rows = from_behind(orbitals[:AHEAD], "orb", -1)
    windows = build_windows(orbitals, upper_rows, count_local, steps_ahead)
    widened = lax.all_to_all(windows, GRID, split_axis=0, concat_axis=1, tiled=True)
    full_rows = widened.shape[1]
    extended = widened.reshape(count_local + AHEAD, B, B, B)
    own_boxes = extended[:count_local]
    first_index = lax.axis_index(ORB_GRID) * count_local
    local_index = jnp.remainder(partners - first_index, total_orbitals)

    def per_orbital(packed):
        own_box, chosen, pair_offsets = packed
        return pair_terms(own_box, extended[chosen], pair_offsets)

    own_force, partner_force = lax.map(per_orbital, (own_boxes, local_index, offsets))
    spread = (
        jnp.zeros_like(extended)
        .at[local_index.reshape(-1)]
        .add(partner_force.reshape((-1,) + extended.shape[1:]))
    )
    kinetic = (-0.5 * apply_operator(own_boxes)).reshape(count_local, full_rows, width_last)
    all_force = jnp.concatenate([own_force + spread[:count_local], spread[count_local:]], axis=0)
    packed_all = (exact_share * all_force).reshape(count_local + AHEAD, full_rows, width_last)
    returned, restored = (
        two_step_exchange(packed_all, (("grid_0", "grid_1"), "grid_2"), (0, 1), 1, 0),
        two_step_exchange(kinetic, (("grid_0", "grid_1"), "grid_2"), (0, 1), 1, 0),
    )
    exchange_force = fold_windows(returned, count_local, steps_ahead)
    advanced = (
        2.0 * orbitals
        - previous
        + verlet_factor * (restored + exchange_force - potential * orbitals)
    )
    return (advanced, exchange_force)


def solution(mesh):
    split = Mesh(
        mesh.devices.reshape(mesh.shape["orb"], 8, 4, 2), ("orb", "grid_0", "grid_1", "grid_2")
    )
    return jax.shard_map(
        local,
        mesh=split,
        in_specs=(
            P("orb", GRID, None),
            P("orb", GRID, None),
            P("orb", GRID, None),
            P(ORB_GRID, None),
            P(ORB_GRID, None, None),
        ),
        out_specs=(P("orb", GRID, None), P("orb", GRID, None)),
        check_vma=False,
    )
```

profile of v0, /device:TPU:2, one launch (start us, length us, event | category | flops | bytes accessed | tf_op | source)
XLA Modules:
  0.0 577.9 jit_solution(16364896627483350653)
XLA Ops:
  9.8 12.2 %all-to-all-start = ((f32[320,32,128]{2,1,0:T(8,128)}), f32[320,32,128]{2,1,0:T(8,128)}, u32[]{:S(2)}, u32[]{:S(2)}) async-start(f32[320,32,128]{2,1,0:T(8,128)} %bitcast.114), calls=%async_computation | async-start | bytes 10485760 | tf_op jit(solution)/shard_map/all_to_all | solution.py:170
  22.4 118.1 %all-to-all-done = f32[320,32,128]{2,1,0:T(8,128)} async-done(((f32[320,32,128]{2,1,0:T(8,128)}), f32[320,32,128]{2,1,0:T(8,128)}, u32[]{:S(2)}, u32[]{:S(2)}) %all-to-all-start) | async-done | bytes 5242912 | tf_op jit(solution)/shard_map/all_to_all | solution.py:170
  140.6 8.5 %reshape.78 = f32[5,64,64,64]{3,2,0,1:T(8,128)} reshape(f32[5,64,32,128]{3,2,0,1:T(8,128)} %bitcast.10) | data formatting | bytes 10485760 | tf_op jit(solution)/shard_map/reshape | solution.py:172
  152.4 7.5 %gather_fusion = f32[3,64,64,64]{3,2,1,0:T(8,128)} fusion(f32[5,64,64,64]{3,2,0,1:T(8,128)} %reshape.78, s32[1024]{0:T(1024)S(1)} %pad_clamp_fusion), kind=kCustom, calls=%fused_computation | custom fusion | bytes 6291468 | tf_op jit(solution)/shard_map/while/body/eval_jaxpr/gather | solution.py:179
  159.9 10.5 %pad.51 = f32[3,96,96,96]{3,2,1,0:T(8,128)} pad(f32[3,64,64,64]{3,2,1,0:T(8,128)} %gather_fusion, f32[]{:T(128)} %constant.49.clone.1), padding=0_0x16_16x16_16x16_16 | pad | bytes 13762564 | tf_op jit(solution)/shard_map/while/body/eval_jaxpr/vmap(jit(_pad))/pad | solution.py:117
  170.4 3.5 broadcast.154.clone
  173.9 20.5 %while.2 = (s32[]{:T(128)}, f32[3,96,96,96]{3,2,1,0:T(8,128)}, s32[3,4]{1,0:T(4,128)S(1)}, f32[3,64,64,64]{3,2,1,0:T(8,128)}, s32[]{:T(128)}) while((s32[]{:T(128)}, f32[3,96,96,96]{3,2,1,0:T(8,128)}, s32[3,4]{1,0:T(4,128)S(1)}, f32[3,64,64,64]{3,2,1,0:T(8,128)}, s32[]{:T(128)}) %tuple.70), condition=%wide.while_cond, body=%wide.while_body.sunk | while | flops 2 | bytes 4196993 | solution.py:119
  174.6 6.2 %dynamic-slice_dynamic-update-slice_fusion.4 = f32[3,64,64,64]{3,2,1,0:T(8,128)} fusion(f32[3,64,64,64]{3,2,1,0:T(8,128)} %get-tuple-element.203, s32[]{:T(128)} %get-tuple-element.200, f32[3,96,96,96]{3,2,1,0:T(8,128)} %get-tuple-element.206, s32[]{:T(128)} %bitcast.104, s32[]{:T(128)} %bitcast.105, s32[]{:T(128)} %bitcast.106, s32[]{:T(128)} %bitcast.107), kind=kLoop, calls=%fused_computation.2.clone.1 | loop fusion | bytes 4196864 | tf_op jit(solution)/shard_map/while/body/eval_jaxpr/vmap()/gather
  181.5 6.1 %dynamic-slice_dynamic-update-slice_fusion.4 = f32[3,64,64,64]{3,2,1,0:T(8,128)} fusion(f32[3,64,64,64]{3,2,1,0:T(8,128)} %get-tuple-element.203, s32[]{:T(128)} %get-tuple-element.200, f32[3,96,96,96]{3,2,1,0:T(8,128)} %get-tuple-element.206, s32[]{:T(128)} %bitcast.104, s32[]{:T(128)} %bitcast.105, s32[]{:T(128)} %bitcast.106, s32[]{:T(128)} %bitcast.107), kind=kLoop, calls=%fused_computation.2.clone.1 | loop fusion | bytes 4196864 | tf_op jit(solution)/shard_map/while/body/eval_jaxpr/vmap()/gather
  188.3 6.2 %dynamic-slice_dynamic-update-slice_fusion.4 = f32[3,64,64,64]{3,2,1,0:T(8,128)} fusion(f32[3,64,64,64]{3,2,1,0:T(8,128)} %get-tuple-element.203, s32[]{:T(128)} %get-tuple-element.200, f32[3,96,96,96]{3,2,1,0:T(8,128)} %get-tuple-element.206, s32[]{:T(128)} %bitcast.104, s32[]{:T(128)} %bitcast.105, s32[]{:T(128)} %bitcast.106, s32[]{:T(128)} %bitcast.107), kind=kLoop, calls=%fused_computation.2.clone.1 | loop fusion | bytes 4196864 | tf_op jit(solution)/shard_map/while/body/eval_jaxpr/vmap()/gather
  194.5 6.9 %multiply_multiply_fusion = f32[3,64,64,64]{3,2,1,0:T(8,128)} fusion(f32[3,64,64,64]{3,2,1,0:T(8,128)} %get-tuple-element.30, f32[64,64,64]{2,1,0:T(8,128)S(1)} %mul.171), kind=kLoop, calls=%fused_computation.93 | loop fusion | flops 1572864 | bytes 7340032 | tf_op jit(solution)/shard_map/while/body/eval_jaxpr/vmap()/div | solution.py:103
  201.3 35.3 %multiply_add_fusion.1 = (f32[3,64,64,64]{3,2,1,0:T(8,128)}, f32[3,64,64,64]{3,2,1,0:T(8,128)}) fusion(f32[3,64,64,64]{3,2,1,0:T(8,128)} %get-tuple-element.30, f32[64,64,64]{2,1,0:T(8,128)S(1)} %mul.171, f32[3,64,64,64]{3,2,1,0:T(8,128)} %multiply_multiply_fusion), kind=kLoop, calls=%fused_computation.92 | loop fusion | flops 16515072 | bytes 13631488 | tf_op jit(solution)/shard_map/while/body/eval_jaxpr/vmap()/add | solution.py:110
  236.6 15.6 %fusion.56 = f32[1,64,64,64]{3,2,1,0:T(8,128)} fusion(f32[1,64,64,64]{3,2,1,0:T(8,128)} %slice.290), kind=kLoop, calls=%fused_computation.116 | loop fusion | flops 4194304 | bytes 2097152 | tf_op jit(solution)/shard_map/mul | solution.py:187
  254.8 5.1 all-to-all-start.1
  259.9 35.4 %multiply_add_fusion = (f32[3,64,64,64]{3,2,1,0:T(8,128)}, f32[3,64,64,64]{3,2,1,0:T(8,128)}) fusion(f32[3,64,64,64]{3,2,1,0:T(8,128)} %get-tuple-element.101, f32[3,64,64,64]{3,2,1,0:T(8,128)} %get-tuple-element.102), kind=kLoop, calls=%fused_computation.91 | loop fusion | flops 14942208 | bytes 12582912 | tf_op jit(solution)/shard_map/while/body/eval_jaxpr/vmap()/add | solution.py:110
  295.3 42.7 %multiply_reduce_fusion = (f32[64,64,64]{2,1,0:T(8,128)}, f32[3,64,64,64]{3,2,1,0:T(8,128)}) fusion(f32[3,64,64,64]{3,2,1,0:T(8,128)} %get-tuple-element.30, f32[3,64,64,64]{3,2,1,0:T(8,128)} %get-tuple-element.100, f32[3,64,64,64]{3,2,1,0:T(8,128)} %get-tuple-element.99, f32[3,64,64,64]{3,2,1,0:T(8,128)} %get-tuple-element.101, f32[64,64,64]{2,1,0:T(8,128)S(1)} %mul.171), kind=kLoop, calls=%fused_computation.90 | loop fusion | flops 20185088 | bytes 17825792 | tf_op jit(solution)/shard_map/while/body/eval_jaxpr/reduce_sum | solution.py:130
  338.0 6.8 %broadcast_multiply_fusion = f32[3,64,64,64]{3,2,1,0:T(8,128)} fusion(f32[3,64,64,64]{3,2,1,0:T(8,128)} %get-tuple-element.98, f32[64,64,64]{2,1,0:T(8,128)S(1)} %mul.171), kind=kLoop, calls=%fused_computation.95 | loop fusion | flops 786432 | bytes 7340032 | tf_op jit(solution)/shard_map/while/body/eval_jaxpr/vmap()/mul | solution.py:127
  344.7 10.5 %pad.55 = f32[3,96,96,96]{3,2,1,0:T(8,128)} pad(f32[3,64,64,64]{3,2,1,0:T(8,128)} %broadcast_multiply_fusion, f32[]{:T(128)} %constant.49.clone.1), padding=0_0x16_16x16_16x16_16 | pad | bytes 13762564 | tf_op jit(solution)/shard_map/while/body/eval_jaxpr/vmap(jit(_pad))/pad | solution.py:117
  355.2 3.4 broadcast.154
  358.6 20.2 %while.3 = (s32[]{:T(128)}, f32[3,96,96,96]{3,2,1,0:T(8,128)}, s32[3,4]{1,0:T(4,128)S(1)}, f32[3,64,64,64]{3,2,1,0:T(8,128)}, s32[]{:T(128)}) while((s32[]{:T(128)}, f32[3,96,96,96]{3,2,1,0:T(8,128)}, s32[3,4]{1,0:T(4,128)S(1)}, f32[3,64,64,64]{3,2,1,0:T(8,128)}, s32[]{:T(128)}) %tuple.73), condition=%wide.while_cond.1, body=%wide.while_body.1.sunk | while | flops 2 | bytes 4196993 | solution.py:119
  359.2 6.1 %dynamic-slice_dynamic-update-slice_fusion.5 = f32[3,64,64,64]{3,2,1,0:T(8,128)} fusion(f32[3,64,64,64]{3,2,1,0:T(8,128)} %get-tuple-element.218, s32[]{:T(128)} %get-tuple-element.215, f32[3,96,96,96]{3,2,1,0:T(8,128)} %get-tuple-element.221, s32[]{:T(128)} %bitcast.108, s32[]{:T(128)} %bitcast.109, s32[]{:T(128)} %bitcast.110, s32[]{:T(128)} %bitcast.111), kind=kLoop, calls=%fused_computation.4.clone.1 | loop fusion | bytes 4196864 | tf_op jit(solution)/shard_map/while/body/eval_jaxpr/vmap()/gather
  366.0 6.1 %dynamic-slice_dynamic-update-slice_fusion.5 = f32[3,64,64,64]{3,2,1,0:T(8,128)} fusion(f32[3,64,64,64]{3,2,1,0:T(8,128)} %get-tuple-element.218, s32[]{:T(128)} %get-tuple-element.215, f32[3,96,96,96]{3,2,1,0:T(8,128)} %get-tuple-element.221, s32[]{:T(128)} %bitcast.108, s32[]{:T(128)} %bitcast.109, s32[]{:T(128)} %bitcast.110, s32[]{:T(128)} %bitcast.111), kind=kLoop, calls=%fused_computation.4.clone.1 | loop fusion | bytes 4196864 | tf_op jit(solution)/shard_map/while/body/eval_jaxpr/vmap()/gather
  372.7 6.1 %dynamic-slice_dynamic-update-slice_fusion.5 = f32[3,64,64,64]{3,2,1,0:T(8,128)} fusion(f32[3,64,64,64]{3,2,1,0:T(8,128)} %get-tuple-element.218, s32[]{:T(128)} %get-tuple-element.215, f32[3,96,96,96]{3,2,1,0:T(8,128)} %get-tuple-element.221, s32[]{:T(128)} %bitcast.108, s32[]{:T(128)} %bitcast.109, s32[]{:T(128)} %bitcast.110, s32[]{:T(128)} %bitcast.111), kind=kLoop, calls=%fused_computation.4.clone.1 | loop fusion | bytes 4196864 | tf_op jit(solution)/shard_map/while/body/eval_jaxpr/vmap()/gather
  378.8 5.3 broadcast_in_dim.31
  384.1 11.9 %scatter_fusion = f32[5,64,64,64]{3,2,1,0:T(8,128)} fusion(f32[5,64,64,64]{3,2,1,0:T(8,128)} %broadcast_in_dim.31, s32[3]{0:T(128)S(1)} %fusion.77, f32[3,64,64,64]{3,2,1,0:T(8,128)} %get-tuple-element.38), kind=kCustom, calls=%fused_computation.1 | custom fusion | flops 786432 | bytes 9437196 | tf_op jit(solution)/shard_map/scatter-add | solution.py:185
  396.1 8.4 %slice.400 = f32[4,64,64,64]{3,2,1,0:T(8,128)} slice(f32[5,64,64,64]{3,2,1,0:T(8,128)} %scatter_fusion), slice={[1:5], [0:64], [0:64], [0:64]} | slice | bytes 8388608 | tf_op jit(solution)/shard_map/slice | solution.py:188
  404.5 7.4 %concatenate.27 = f32[4,64,32,128]{3,2,1,0:T(8,128)} reshape(f32[4,64,64,64]{3,2,1,0:T(8,128)} %slice.400) | data formatting | bytes 8388608 | tf_op jit(solution)/shard_map/concatenate | solution.py:188
  422.8 4.6 all_to_all.35
  427.4 9.8 %all-to-all-start.3 = ((f32[32,2,5,32,128]{4,3,1,2,0:T(8,128)}), f32[32,2,5,32,128]{4,3,1,2,0:T(8,128)}, u32[]{:S(2)}, u32[]{:S(2)}) async-start(f32[32,2,5,32,128]{4,3,1,2,0:T(8,128)} %copy.75), calls=%async_computation.3 | async-start | bytes 10485760 | tf_op jit(solution)/shard_map/all_to_all | solution.py:43
  437.3 120.5 %all-to-all-done.3 = f32[32,2,5,32,128]{4,3,1,2,0:T(8,128)} async-done(((f32[32,2,5,32,128]{4,3,1,2,0:T(8,128)}), f32[32,2,5,32,128]{4,3,1,2,0:T(8,128)}, u32[]{:S(2)}, u32[]{:S(2)}) %all-to-all-start.3) | async-done | bytes 5242912 | tf_op jit(solution)/shard_map/all_to_all | solution.py:43
  560.9 7.9 %all_to_all.36 = f32[32,2,5,32,128]{4,3,0,2,1:T(8,128)S(1)} all-to-all(f32[32,2,5,32,128]{4,3,0,2,1:T(8,128)S(1)} %copy.76), channel_id=1, replica_groups=mesh['orb'=4,'grid_0'=8,'grid_1'=4,'grid_2'=2] {'grid_2'}, dimensions={1} | all-to-all | bytes 10485760 | tf_op jit(solution)/shard_map/all_to_all | solution.py:43
  571.4 4.7 collective-permute-done.1
  (64 shorter events, 37.9 us)
Async XLA Ops:
  1.5 5.6 collective-permute-start
  7.3 14.6 %copy-start.5 = (s32[1,3,3]{2,0,1:T(1,128)S(1)}, s32[1,3,3]{2,0,1:T(1,128)}, u32[]{:S(2)}) copy-start(s32[1,3,3]{2,0,1:T(1,128)} %param.9) | copy-start | bytes 112
  7.4 15.0 %copy-start.6 = (s32[1,3]{1,0:T(1,128)S(1)}, s32[1,3]{1,0:T(1,128)}, u32[]{:S(2)}) copy-start(s32[1,3]{1,0:T(1,128)} %param.8) | copy-start | bytes 40
  7.4 2.3 copy-start.2
  9.8 130.8 %all-to-all-start = ((f32[320,32,128]{2,1,0:T(8,128)}), f32[320,32,128]{2,1,0:T(8,128)}, u32[]{:S(2)}, u32[]{:S(2)}) async-start(f32[320,32,128]{2,1,0:T(8,128)} %bitcast.114), calls=%async_computation | async-start | bytes 10485760 | tf_op jit(solution)/shard_map/all_to_all | solution.py:170
  254.8 167.9 %all-to-all-start.1 = ((f32[32,2,1,32,128]{4,3,1,2,0:T(8,128)}), f32[32,2,1,32,128]{4,3,1,2,0:T(8,128)S(1)}, u32[]{:S(2)}, u32[]{:S(2)}) async-start(f32[32,2,1,32,128]{4,3,1,2,0:T(8,128)} %reshape_transpose_reshape_reshape.3), calls=%async_computation.1 | async-start | bytes 2097152 | tf_op jit(solution)/shard_map/all_to_all | solution.py:43
  404.5 7.4 %copy-start.1 = (f32[64,64,64]{2,1,0:T(8,128)S(1)}, f32[64,64,64]{2,1,0:T(8,128)}, u32[]{:S(2)}) copy-start(f32[64,64,64]{2,1,0:T(8,128)} %get-tuple-element.97) | copy-start | bytes 3145732
  427.4 130.4 %all-to-all-start.3 = ((f32[32,2,5,32,128]{4,3,1,2,0:T(8,128)}), f32[32,2,5,32,128]{4,3,1,2,0:T(8,128)}, u32[]{:S(2)}, u32[]{:S(2)}) async-start(f32[32,2,5,32,128]{4,3,1,2,0:T(8,128)} %copy.75), calls=%async_computation.3 | async-start | bytes 10485760 | tf_op jit(solution)/shard_map/all_to_all | solution.py:43
  570.5 5.6 copy-start
  570.5 5.6 copy-start.3
  570.5 5.6 copy-start.4
  570.6 5.6 collective-permute-start.1
where the time goes:
time: 580 us; the launch traced here: 578 us
  waiting for transfers between devices  243 us (42%)
  other arithmetic  163 us (28%)
  local copies, waits for them, and re-layouts  128 us (22%)
  starting transfers between devices  30.3 us (5%)
  blocking collectives  12.5 us (2%)
    all_to_all x2, waiting for transfers between devices, exchange_in_order(): out = lax.all_to_all(out, axes[k], k, k, tiled=True)  121 us
    all_to_all x1, waiting for transfers between devices, local(): lax.all_to_all(windows, GRID, split_axis=0, concat_axis=1, tiled=True)  118 us
    add x2, other arithmetic, solve_potential(): direction = keep_weight * direction + residual_weight * residual  70.7 us
    reduce_sum x1, other arithmetic, pair_terms(): return (jnp.sum(own_terms, axis=0), partner_terms)  42.7 us
    gather x18, local copies, waits for them, and re-layouts  40.7 us
    pad x2, local copies, waits for them, and re-layouts, shift_box(): padded = jnp.pad(one_box, reach_cells)  21 us
    mul x1, other arithmetic, local(): -0.5 * apply_operator(own_boxes)  15.6 us
    all_to_all x2, starting transfers between devices, exchange_in_order(): out = lax.all_to_all(out, axes[k], k, k, tiled=True)  14.8 us
  transfers between devices with their start and end apart: 5, of which 3 were waited for; matrix products, arithmetic and copies ran while one was open for 29% of the time, Pallas kernels for 0%

commit v1 on v0

v1 whole, which is shorter than its diff:
```python
import functools

import jax
import jax.numpy as jnp
import numpy as np
from jax import lax
from jax.experimental import pallas as pl
from jax.experimental.pallas import tpu as pltpu
from jax.sharding import PartitionSpec as P

B = 64
SWEEPS = 4
AHEAD = 4
HALF = B // 2
LANES = 2 * B
PAD = 8
HIGH = HALF + 2 * PAD
DEEP = B + 4

coulomb_factor = 4.0 * np.pi
exact_share = 0.25
verlet_factor = 0.05
lower_edge = 0.5
upper_edge = 16.0


def sweep_polynomial():
    centre = 0.5 * (upper_edge + lower_edge)
    radius = 0.5 * (upper_edge - lower_edge)
    sigma = centre / radius
    operator = np.polynomial.Polynomial([centre, radius])
    residual = np.polynomial.Polynomial([coulomb_factor])
    direction = residual / centre
    total = np.polynomial.Polynomial([0.0])
    rho = 1.0 / sigma
    for turn in range(SWEEPS):
        total = total + direction
        residual = residual - operator * direction
        if turn + 1 < SWEEPS:
            following = 1.0 / (2.0 * sigma - rho)
            direction = following * rho * direction + (2.0 * following / radius) * residual
            rho = following
    return centre, radius, [float(c) for c in total.coef]


def lane_masks(rows):
    lane = lax.broadcasted_iota(jnp.int32, (rows, LANES), 1)
    cell = lane & (B - 1)
    return {
        "upper": lane >= B,
        "last": cell < B - 1,
        "first": cell > 0,
        "last2": cell < B - 2,
        "first2": cell > 1,
        "cell": cell,
    }


def stencil_plane(ref, a, masks, weights):
    mid = a + 2
    here = ref[mid, PAD : PAD + HALF, :]
    below = ref[mid, PAD - 1 : PAD - 1 + HALF, :]
    above = ref[mid, PAD + 1 : PAD + 1 + HALF, :]

    def turned(by, mask):
        return jnp.where(mask, pltpu.roll(here, by % LANES, 1), 0.0)

    swapped = pltpu.roll(here + jnp.where(masks["upper"], below, above), B, 1)
    near = (
        swapped
        + (ref[mid - 1, PAD : PAD + HALF, :] + ref[mid + 1, PAD : PAD + HALF, :])
        + (turned(-1, masks["last"]) + turned(1, masks["first"]))
    )
    far = (
        (below + above)
        + (ref[mid - 2, PAD : PAD + HALF, :] + ref[mid + 2, PAD : PAD + HALF, :])
        + (turned(-2, masks["last2"]) + turned(2, masks["first2"]))
    )
    return weights[0] * here + weights[1] * near + weights[2] * far


def clear_edges(ref):
    deep = ref.shape[0]
    zero = jnp.zeros((PAD, LANES), jnp.float32)

    def one(a, carry):
        ref[a, :PAD, :] = zero
        ref[a, PAD + HALF :, :] = zero
        return carry

    lax.fori_loop(0, deep, one, 0, unroll=4)
    if deep == DEEP:
        for a in (0, 1, DEEP - 2, DEEP - 1):
            ref[a] = jnp.zeros((HIGH, LANES), jnp.float32)


def inner_rows(ref):
    lead = (ref.shape[0] - B) // 2
    return ref.at[pl.ds(lead, B), pl.ds(PAD, HALF), :]


def kinetic_kernel(boxes, out_ref, box, sem):
    copy = pltpu.make_async_copy(boxes.at[:, 0], inner_rows(box), sem)
    copy.start()
    clear_edges(box)
    copy.wait()
    masks = lane_masks(HALF)
    weights = (-0.5 * 7.5, 0.5 * 4.0 / 3.0, -0.5 / 12.0)

    def one(a, carry):
        out_ref[a] = stencil_plane(box, a, masks, weights)
        return carry

    lax.fori_loop(0, B, one, 0, unroll=2)


def shifted_plane(ref, a, offset, masks):
    lead = (ref.shape[0] - B) // 2
    o0, o1, o2 = offset
    half = lax.shift_right_arithmetic(o1, 1)
    odd = o1 & 1
    source = a + o0
    inside = jnp.logical_and(source >= 0, source < B)
    source = jnp.clip(source, 0, B - 1) + lead
    low = ref[source, pl.ds(PAD + half, HALF), :]
    high = ref[source, pl.ds(PAD + half + odd, HALF), :]
    mixed = jnp.where(masks["upper"] == (odd == 1), low, high)
    turned = pltpu.roll(mixed, (2 * LANES - o2 - B * odd) & (LANES - 1), 1)
    reached = masks["cell"] + o2
    keep = jnp.logical_and(jnp.logical_and(reached >= 0, reached < B), inside)
    return jnp.where(keep, turned, 0.0)


def pairs_kernel(dist, offs, boxes, peers, kept, sent, own, near, rho, work_a, work_b, moved, force, sems, out_sem):
    own_copy = pltpu.make_async_copy(boxes.at[:, 0], own, sems.at[3])
    own_copy.start()
    sources = {1: peers.at[:, 0], 2: boxes.at[:, 1], 3: peers.at[:, 1], 4: boxes.at[:, 2]}

    def fetch(source, q):
        pltpu.make_async_copy(source, inner_rows(near.at[q]), sems.at[q]).start()

    for q in range(3):
        for far, source in sources.items():
            pl.when(dist[q] == far)(functools.partial(fetch, source, q))
    for q in range(3):
        clear_edges(near.at[q])
    for buffer in (rho, work_a, work_b):
        clear_edges(buffer)
    masks = lane_masks(HALF)
    centre, radius, poly = sweep_polynomial()
    poly = [exact_share * c for c in poly]
    step = ((7.5 - centre) / radius, -4.0 / 3.0 / radius, 1.0 / 12.0 / radius)
    first = tuple(poly[3] * s for s in step)
    rows = pl.ds(PAD, HALF)
    absent = 10 - dist[0] - dist[1] - dist[2]

    def blank(a, carry):
        force[absent, a] = jnp.zeros((HALF, LANES), jnp.float32)
        return carry

    lax.fori_loop(0, B, blank, 0, unroll=4)
    own_copy.wait()
    for q in range(3):
        offset = (offs[3 * q], offs[3 * q + 1], offs[3 * q + 2])
        back = tuple(-o for o in offset)
        partner = near.at[q]
        target = dist[q]
        pltpu.make_async_copy(boxes.at[:, 0], inner_rows(partner), sems.at[q]).wait()

        def overlap(a, carry):
            there = shifted_plane(partner, a, offset, masks)
            moved[a] = there
            rho[a + 2, rows, :] = own[a] * there
            return carry

        def sweep_one(a, carry):
            work_a[a + 2, rows, :] = stencil_plane(rho, a, masks, first) + poly[2] * rho[a + 2, rows, :]
            return carry

        def sweep_two(a, carry):
            work_b[a + 2, rows, :] = stencil_plane(work_a, a, masks, step) + poly[1] * rho[a + 2, rows, :]
            return carry

        def sweep_three(a, carry):
            found = stencil_plane(work_b, a, masks, step) + poly[0] * rho[a + 2, rows, :]
            term = found * moved[a]
            force[0, a] = term if q == 0 else force[0, a] + term
            work_a[a + 2, rows, :] = found * own[a]
            return carry

        def give(a, carry):
            force[target, a] = shifted_plane(work_a, a, back, masks)
            return carry

        for body in (overlap, sweep_one, sweep_two, sweep_three, give):
            lax.fori_loop(0, B, body, 0, unroll=2)
    ends = (kept.at[:, 0], sent.at[:, 0], kept.at[:, 1], sent.at[:, 1], kept.at[:, 2])
    copies = [pltpu.make_async_copy(force.at[k], end, out_sem.at[k]) for k, end in enumerate(ends)]
    for copy in copies:
        copy.start()
    for copy in copies:
        copy.wait()


F32 = jnp.float32
ANY = pl.BlockSpec(memory_space=pl.ANY)
SCALARS = pl.BlockSpec(memory_space=pltpu.SMEM)


def kinetic_of(boxes):
    return pl.pallas_call(
        kinetic_kernel,
        out_shape=jax.ShapeDtypeStruct((B, HALF, LANES), F32),
        in_specs=[ANY],
        out_specs=pl.BlockSpec(memory_space=pltpu.VMEM),
        scratch_shapes=[pltpu.VMEM((DEEP, HIGH, LANES), F32), pltpu.SemaphoreType.DMA],
        cost_estimate=pl.CostEstimate(flops=20 * B**3, transcendentals=0, bytes_accessed=8 * B**3),
        name="kinetic",
    )(boxes)


def pair_forces(dist, offs, boxes, peers):
    padded = pltpu.VMEM((DEEP, HIGH, LANES), F32)
    return pl.pallas_call(
        pairs_kernel,
        out_shape=[
            jax.ShapeDtypeStruct((B, 3, HALF, LANES), F32),
            jax.ShapeDtypeStruct((B, 2, HALF, LANES), F32),
        ],
        in_specs=[SCALARS, SCALARS, ANY, ANY],
        out_specs=[ANY, ANY],
        scratch_shapes=[
            pltpu.VMEM((B, HALF, LANES), F32),
            pltpu.VMEM((3, B, HIGH, LANES), F32),
            padded,
            padded,
            padded,
            pltpu.VMEM((B, HALF, LANES), F32),
            pltpu.VMEM((5, B, HALF, LANES), F32),
            pltpu.SemaphoreType.DMA((4,)),
            pltpu.SemaphoreType.DMA((5,)),
        ],
        cost_estimate=pl.CostEstimate(flops=300 * B**3, transcendentals=0, bytes_accessed=40 * B**3),
        name="pairs",
    )(dist, offs, boxes, peers)


def from_behind(array, axis, by):
    count = lax.axis_size(axis)
    return lax.ppermute(array, axis, [(i, (i + by) % count) for i in range(count)])


def core_swap(array):
    count = lax.axis_size("grid")
    return lax.ppermute(array, "grid", [(i, i ^ 1) for i in range(count)])


def local(orbitals, previous, potential, partners, offsets):
    slabs = lax.axis_size("grid")
    total = lax.axis_size("orb") * slabs
    place = lax.axis_index(("orb", "grid"))
    core = place & 1
    dist = jnp.remainder(partners[0] - place, total)
    offs = offsets.reshape(-1)

    upper = from_behind(orbitals[:AHEAD], "orb", -1)
    longer = jnp.concatenate([orbitals, upper], axis=0)
    windows = jnp.stack([longer[:slabs], longer[2 : 2 + slabs], longer[4 : 4 + slabs]], axis=1)
    boxes = lax.all_to_all(windows, "grid", split_axis=0, concat_axis=0, tiled=True)
    offered = lax.dynamic_slice_in_dim(boxes, 1 - core, 2, axis=1)
    peers = core_swap(offered)
    kinetic = lax.all_to_all(kinetic_of(boxes), "grid", split_axis=0, concat_axis=0, tiled=True)

    kept, sent = pair_forces(dist, offs, boxes, peers)
    given = core_swap(sent)
    even = core == 0
    zero = jnp.zeros_like(given[:, 0])
    summed = kept + jnp.stack(
        [
            jnp.where(even, zero, given[:, 0]),
            jnp.where(even, given[:, 0], given[:, 1]),
            jnp.where(even, given[:, 1], zero),
        ],
        axis=1,
    )
    returned = lax.all_to_all(summed, "grid", split_axis=0, concat_axis=0, tiled=True)
    own, two, four = returned[:, 0], returned[:, 1], returned[:, 2]
    spill = four[slabs - 4 :] + jnp.pad(two[slabs - 2 :], ((0, 2), (0, 0), (0, 0)))
    spill = from_behind(spill, "orb", 1)
    exchange_force = own + jnp.concatenate(
        [spill[:2], spill[2:] + two[:2], two[2 : slabs - 2] + four[: slabs - 4]], axis=0
    )
    advanced = (
        2.0 * orbitals
        - previous
        + verlet_factor * (kinetic + exchange_force - potential * orbitals)
    )
    return advanced, exchange_force


def solution(mesh):
    rows = P("orb", "grid", None)
    return jax.shard_map(
        local,
        mesh=mesh,
        in_specs=(rows, rows, rows, P(("orb", "grid"), None), P(("orb", "grid"), None, None)),
        out_specs=(rows, rows),
        check_vma=False,
    )
```

time: 580 us -> 282 us (0.49)
  other arithmetic: 163 us -> 12.7 us
  local copies, waits for them, and re-layouts: 128 us -> 4.79 us
  waiting for transfers between devices: 243 us -> 176 us
  Pallas kernels: 0 us -> 59.1 us
  blocking collectives: 12.5 us -> 0 us
    all_to_all x3, waiting for transfers between devices: 239 us -> 164 us  [the longest x1 73.7 us: local(): lax.all_to_all(windows, 'grid', split_axis=0, concat_axis=0, tiled=True)]
    add x5 -> x3, other arithmetic: 74.6 us -> 3.62 us  [the longest x1 2.45 us: local(): kept + jnp.stack([jnp.where(even, zero, given[:, 0]), jnp.where(even, giv...]
    pallas_call x0 -> x2, Pallas kernels: none -> 59.1 us  [the longest x1 53.3 us: pair_forces(): pl.pallas_call(pairs_kernel, out_shape=[jax.ShapeDtypeStruct((B, 3, HALF,...]
    gather x19 -> x0, local copies, waits for them, and re-layouts: 48.2 us -> none
    reduce_sum x1 -> x0, other arithmetic: 42.7 us -> none  [pair_terms(): return (jnp.sum(own_terms, axis=0), partner_terms)]
    mul x3 -> x0, other arithmetic: 25.2 us -> none  [the longest x1 15.6 us: local(): -0.5 * apply_operator(own_boxes)]
    pad x2 -> x0, local copies, waits for them, and re-layouts: 21 us -> none  [shift_box(): padded = jnp.pad(one_box, reach_cells)]
    all_to_all x2 -> x0, blocking collectives: 12.5 us -> none  [exchange_in_order(): out = lax.all_to_all(out, axes[k], k, k, tiled=True)]
  transfers between devices with their start and end apart: 5 -> 7, of which waited for: 3 -> 7; matrix products, arithmetic and copies ran while one was open for 29% -> 1% of each run, Pallas kernels for 0% -> 2%
where the time goes in v1:
time: 282 us; the launch traced here: 281 us
  waiting for transfers between devices  176 us (62%)
  Pallas kernels  59.1 us (21%)
  starting transfers between devices  27.3 us (10%)
  other arithmetic  12.7 us (5%)
  local copies, waits for them, and re-layouts  4.79 us (2%)
    all_to_all x1, waiting for transfers between devices, local(): lax.all_to_all(windows, 'grid', split_axis=0, concat_axis=0, tiled=True)  73.7 us
    all_to_all x1, waiting for transfers between devices, local(): lax.all_to_all(summed, 'grid', split_axis=0, concat_axis=0, tiled=True)  67.9 us
    pallas_call x1, Pallas kernels, pair_forces(): pl.pallas_call(pairs_kernel, out_shape=[jax.ShapeDtypeStruct((B, 3, HALF,...  53.3 us
    all_to_all x1, waiting for transfers between devices, local(): lax.all_to_all(kinetic_of(boxes), 'grid', split_axis=0, concat_axis=0, ti...  22.6 us
    all_to_all x1, starting transfers between devices, local(): lax.all_to_all(windows, 'grid', split_axis=0, concat_axis=0, tiled=True)  12 us
    ppermute x2, waiting for transfers between devices, core_swap(): return lax.ppermute(array, 'grid', [(i, i ^ 1) for i in range(count)])  7.72 us
    pallas_call x1, Pallas kernels, kinetic_of(): pl.pallas_call(kinetic_kernel, out_shape=jax.ShapeDtypeStruct((B, HALF, L...  5.84 us
  transfers between devices with their start and end apart: 7, of which 7 were waited for; matrix products, arithmetic and copies ran while one was open for 1% of the time, Pallas kernels for 2%

profile of v1, /device:TPU:2, one launch (start us, length us, event | category | flops | bytes accessed | tf_op | source)
XLA Modules:
  0.0 281.0 jit_solution(12455926777791177898)
XLA Ops:
  0.6 0.8 slice.59
  1.5 3.0 %collective-permute-start = (f32[4,32,128]{2,1,0:T(8,128)S(1)}, f32[4,32,128]{2,1,0:T(8,128)S(1)}, u32[]{:S(2)}, u32[]{:S(2)}) collective-permute-start(f32[4,32,128]{2,1,0:T(8,128)S(1)} %slice.59), channel_id=1, source_target_pairs={{0,192},{64,0},{128,64},{192,128},{1,193},{65,1},{129,65},{193,129... | collective-permute-start | bytes 196616 | tf_op jit(solution)/shard_map/ppermute | solution.py:250
  4.5 1.3 constant_dynamic-update-slice_fusion.1
  5.8 0.6 collective-permute-done
  6.4 0.2 slice_bitcast_fusion.2
  6.7 0.0 copy-done.1
  6.7 2.0 pad_maximum_fusion
  8.6 12.0 %all-to-all-start = ((f32[64,3,32,128]{3,2,1,0:T(8,128)}), f32[64,3,32,128]{3,2,1,0:T(8,128)S(1)}, u32[]{:S(2)}, u32[]{:S(2)}) async-start(f32[64,3,32,128]{3,2,1,0:T(8,128)} %pad_maximum_fusion), calls=%async_computation | async-start | bytes 6291456 | tf_op jit(solution)/shard_map/all_to_all | solution.py:269
  20.7 0.0 copy-start.3
  20.7 0.0 copy-start.4
  20.7 73.7 %all-to-all-done.boxes = f32[64,3,32,128]{3,2,1,0:T(8,128)S(1)} async-done(((f32[64,3,32,128]{3,2,1,0:T(8,128)}), f32[64,3,32,128]{3,2,1,0:T(8,128)S(1)}, u32[]{:S(2)}, u32[]{:S(2)}) %all-to-all-start) | async-done | bytes 3145760 | tf_op jit(solution)/shard_map/all_to_all | solution.py:269
  94.4 1.8 constant_dynamic-slice_fusion
  96.1 0.0 collective-permute-start.1
  96.1 0.0 copy-done.3
  96.2 0.6 reshape.15.offs
  96.8 0.0 copy-done.4
  96.8 0.5 and_select_fusion.dist
  97.3 3.4 %collective-permute-done.1.peers = f32[64,2,32,128]{3,2,1,0:T(8,128)} collective-permute-done((f32[64,2,32,128]{3,2,1,0:T(8,128)}, f32[64,2,32,128]{3,2,1,0:T(8,128)}, u32[]{:S(2)}, u32[]{:S(2)}) %collective-permute-start.1) | collective-permute-done | bytes 2097184 | tf_op jit(solution)/shard_map/ppermute | solution.py:255
  100.6 53.3 %pairs.1 = (f32[64,3,32,128]{3,2,1,0:T(8,128)}, f32[64,2,32,128]{3,2,1,0:T(8,128)}) custom-call(s32[3]{0:T(128)} %and_select_fusion.dist, s32[9]{0:T(128)} %reshape.15.offs, f32[64,3,32,128]{3,2,1,0:T(8,128)} %copy-done, f32[64,2,32,128]{3,2,1,0:T(8,128)} %collective-permute-done.1.peers), custom_call_target="tpu_custom_call" | custom-call | flops 78643200 | bytes 10485760 | tf_op jit(solution)/shard_map/pairs/pallas_call | solution.py:224
  153.9 0.2 collective-permute-start.2
  154.2 4.4 %collective-permute-done.2 = f32[64,2,32,128]{3,2,1,0:T(8,128)} collective-permute-done((f32[64,2,32,128]{3,2,1,0:T(8,128)}, f32[64,2,32,128]{3,2,1,0:T(8,128)}, u32[]{:S(2)}, u32[]{:S(2)}) %collective-permute-start.2) | collective-permute-done | bytes 2097184 | tf_op jit(solution)/shard_map/ppermute | solution.py:255
  158.5 2.0 slice_select_fusion.2
  160.6 2.4 maximum_add_fusion
  163.0 5.4 %all-to-all-start.2 = ((f32[64,3,32,128]{3,2,1,0:T(8,128)}), f32[64,3,32,128]{3,2,1,0:T(8,128)S(1)}, u32[]{:S(2)}, u32[]{:S(2)}) async-start(f32[64,3,32,128]{3,2,1,0:T(8,128)} %maximum_add_fusion), calls=%async_computation.2 | async-start | bytes 6291456 | tf_op jit(solution)/shard_map/all_to_all | solution.py:286
  168.5 5.8 %kinetic.1 = f32[64,32,128]{2,1,0:T(8,128)} custom-call(f32[64,3,32,128]{3,2,1,0:T(8,128)} %copy-done), custom_call_target="tpu_custom_call" | custom-call | flops 5242880 | bytes 2097152 | tf_op jit(solution)/shard_map/kinetic/pallas_call | solution.py:211
  174.3 67.9 %all-to-all-done.2 = f32[64,3,32,128]{3,2,1,0:T(8,128)S(1)} async-done(((f32[64,3,32,128]{3,2,1,0:T(8,128)}), f32[64,3,32,128]{3,2,1,0:T(8,128)S(1)}, u32[]{:S(2)}, u32[]{:S(2)}) %all-to-all-start.2) | async-done | bytes 3145760 | tf_op jit(solution)/shard_map/all_to_all | solution.py:286
  242.2 5.6 %all-to-all-start.1 = ((f32[64,32,128]{2,1,0:T(8,128)}), f32[64,32,128]{2,1,0:T(8,128)}, u32[]{:S(2)}, u32[]{:S(2)}) async-start(f32[64,32,128]{2,1,0:T(8,128)} %kinetic.1), calls=%async_computation.1 | async-start | bytes 2097152 | tf_op jit(solution)/shard_map/all_to_all | solution.py:272
  247.8 1.0 collective-permute-start.3
  248.8 1.2 fusion.1
  250.0 3.9 %collective-permute-done.3 = f32[4,32,128]{2,1,0:T(8,128)S(1)} collective-permute-done((f32[4,32,128]{2,1,0:T(8,128)S(1)}, f32[4,32,128]{2,1,0:T(8,128)S(1)}, u32[]{:S(2)}, u32[]{:S(2)}) %collective-permute-start.3) | collective-permute-done | bytes 65568 | tf_op jit(solution)/shard_map/ppermute | solution.py:250
  253.9 22.6 %all-to-all-done.1 = f32[64,32,128]{2,1,0:T(8,128)} async-done(((f32[64,32,128]{2,1,0:T(8,128)}), f32[64,32,128]{2,1,0:T(8,128)}, u32[]{:S(2)}, u32[]{:S(2)}) %all-to-all-start.1) | async-done | bytes 1048608 | tf_op jit(solution)/shard_map/all_to_all | solution.py:272
  276.5 4.5 %multiply_add_fusion = (f32[64,32,128]{2,1,0:T(8,128)}, f32[64,32,128]{2,1,0:T(8,128)}) fusion(f32[64,32,128]{2,1,0:T(8,128)} %param.7, f32[64,32,128]{2,1,0:T(8,128)} %param.5, f32[64,32,128]{2,1,0:T(8,128)} %all-to-all-done.1, f32[64,32,128]{2,1,0:T(8,128)} %param.6, f32[60,32,128]{2,1,0:T(8,128)} %fusion.1, f32[2,32,128]{2,1,0:T(8,128)S(1)} %get-tuple-element.14, ...), kind=kLoop, calls=%fused_computation.6 | loop fusion | flops 2621440 | bytes 8388608 | tf_op jit(solution)/shard_map/add | solution.py:294
  (10 shorter events, 0.1 us)
Async XLA Ops:
  1.5 5.2 %copy-start.1 = (f32[64,32,128]{2,1,0:T(8,128)S(1)}, f32[64,32,128]{2,1,0:T(8,128)}, u32[]{:S(2)}) copy-start(f32[64,32,128]{2,1,0:T(8,128)} %param.5) | copy-start | bytes 3145732
  1.5 4.9 %collective-permute-start = (f32[4,32,128]{2,1,0:T(8,128)S(1)}, f32[4,32,128]{2,1,0:T(8,128)S(1)}, u32[]{:S(2)}, u32[]{:S(2)}) collective-permute-start(f32[4,32,128]{2,1,0:T(8,128)S(1)} %slice.59), channel_id=1, source_target_pairs={{0,192},{64,0},{128,64},{192,128},{1,193},{65,1},{129,65},{193,129... | collective-permute-start | bytes 196616 | tf_op jit(solution)/shard_map/ppermute | solution.py:250
  8.6 85.7 %all-to-all-start = ((f32[64,3,32,128]{3,2,1,0:T(8,128)}), f32[64,3,32,128]{3,2,1,0:T(8,128)S(1)}, u32[]{:S(2)}, u32[]{:S(2)}) async-start(f32[64,3,32,128]{3,2,1,0:T(8,128)} %pad_maximum_fusion), calls=%async_computation | async-start | bytes 6291456 | tf_op jit(solution)/shard_map/all_to_all | solution.py:269
  20.7 75.5 %copy-start.3 = (s32[1,3,3]{2,0,1:T(1,128)S(1)}, s32[1,3,3]{2,0,1:T(1,128)}, u32[]{:S(2)}) copy-start(s32[1,3,3]{2,0,1:T(1,128)} %param.9) | copy-start | bytes 112
  20.7 76.1 %copy-start.4 = (s32[1,3]{1,0:T(1,128)S(1)}, s32[1,3]{1,0:T(1,128)}, u32[]{:S(2)}) copy-start(s32[1,3]{1,0:T(1,128)} %param.8) | copy-start | bytes 40
  94.4 6.3 %copy-start = (f32[64,3,32,128]{3,2,1,0:T(8,128)}, f32[64,3,32,128]{3,2,1,0:T(8,128)S(1)}, u32[]{:S(2)}) copy-start(f32[64,3,32,128]{3,2,1,0:T(8,128)S(1)} %all-to-all-done.boxes) | copy-start | bytes 9437188
  96.1 4.5 %collective-permute-start.1 = (f32[64,2,32,128]{3,2,1,0:T(8,128)}, f32[64,2,32,128]{3,2,1,0:T(8,128)}, u32[]{:S(2)}, u32[]{:S(2)}) collective-permute-start(f32[64,2,32,128]{3,2,1,0:T(8,128)} %constant_dynamic-slice_fusion), channel_id=1, source_target_pairs={{0,1},{1,0},{2,3},{3,2},{4,5},{5,4},{6,7},{7,6},{8,9},{9,8},{10,11... | collective-permute-start | bytes 6291464 | tf_op jit(solution)/shard_map/ppermute | solution.py:255
  153.9 6.6 %copy-start.2 = (f32[64,3,32,128]{3,2,1,0:T(8,128)S(1)}, f32[64,3,32,128]{3,2,1,0:T(8,128)}, u32[]{:S(2)}) copy-start(f32[64,3,32,128]{3,2,1,0:T(8,128)} %get-tuple-element.4) | copy-start | bytes 9437188
  153.9 4.6 %collective-permute-start.2 = (f32[64,2,32,128]{3,2,1,0:T(8,128)}, f32[64,2,32,128]{3,2,1,0:T(8,128)}, u32[]{:S(2)}, u32[]{:S(2)}) collective-permute-start(f32[64,2,32,128]{3,2,1,0:T(8,128)} %get-tuple-element.5), channel_id=1, source_target_pairs={{0,1},{1,0},{2,3},{3,2},{4,5},{5,4},{6,7},{7,6},{8,9},{9,8},{10,11... | collective-permute-start | bytes 6291464 | tf_op jit(solution)/shard_map/ppermute | solution.py:255
  163.0 79.1 %all-to-all-start.2 = ((f32[64,3,32,128]{3,2,1,0:T(8,128)}), f32[64,3,32,128]{3,2,1,0:T(8,128)S(1)}, u32[]{:S(2)}, u32[]{:S(2)}) async-start(f32[64,3,32,128]{3,2,1,0:T(8,128)} %maximum_add_fusion), calls=%async_computation.2 | async-start | bytes 6291456 | tf_op jit(solution)/shard_map/all_to_all | solution.py:286
  242.2 34.3 %all-to-all-start.1 = ((f32[64,32,128]{2,1,0:T(8,128)}), f32[64,32,128]{2,1,0:T(8,128)}, u32[]{:S(2)}, u32[]{:S(2)}) async-start(f32[64,32,128]{2,1,0:T(8,128)} %kinetic.1), calls=%async_computation.1 | async-start | bytes 2097152 | tf_op jit(solution)/shard_map/all_to_all | solution.py:272
  247.8 6.0 %collective-permute-start.3 = (f32[4,32,128]{2,1,0:T(8,128)S(1)}, f32[4,32,128]{2,1,0:T(8,128)S(1)}, u32[]{:S(2)}, u32[]{:S(2)}) collective-permute-start(f32[4,32,128]{2,1,0:T(8,128)S(1)} %fusion.2), channel_id=1, source_target_pairs={{0,64},{64,128},{128,192},{192,0},{1,65},{65,129},{129,193},{193,1... | collective-permute-start | bytes 196616 | tf_op jit(solution)/shard_map/ppermute | solution.py:250

commit v2 on v1

v2 whole, which is shorter than its diff:
```python
import functools

import jax
import jax.numpy as jnp
import numpy as np
from jax import lax
from jax.experimental import pallas as pl
from jax.experimental.pallas import tpu as pltpu
from jax.sharding import PartitionSpec as P


B = 64
SWEEPS = 4
AHEAD = 4
HALF = B // 2
LANES = 2 * B
PAD = 8
HIGH = HALF + 2 * PAD
DEEP = B + 4
SPAN = 32

coulomb_factor = 4.0 * np.pi
exact_share = 0.25
verlet_factor = 0.05
lower_edge = 0.5
upper_edge = 16.0


def sweep_polynomial():
    centre = 0.5 * (upper_edge + lower_edge)
    radius = 0.5 * (upper_edge - lower_edge)
    sigma = centre / radius
    operator = np.polynomial.Polynomial([centre, radius])
    residual = np.polynomial.Polynomial([coulomb_factor])
    direction = residual / centre
    total = np.polynomial.Polynomial([0.0])
    rho = 1.0 / sigma
    for turn in range(SWEEPS):
        total = total + direction
        residual = residual - operator * direction
        if turn + 1 < SWEEPS:
            following = 1.0 / (2.0 * sigma - rho)
            direction = following * rho * direction + (2.0 * following / radius) * residual
            rho = following
    return centre, radius, [float(c) for c in total.coef]


def lane_mixers():
    along = np.zeros((LANES, LANES), np.float32)
    across = np.zeros((LANES, LANES), np.float32)
    for lane in range(LANES):
        half, cell = divmod(lane, B)
        for by, weight in ((1, -16.0), (-1, -16.0), (2, 1.0), (-2, 1.0)):
            if 0 <= cell + by < B:
                along[half * B + cell + by, lane] = weight
        across[(1 - half) * B + cell, lane] = -16.0
    return jnp.asarray(np.concatenate([along, along, across, across], axis=0), jnp.bfloat16)


def halves(x):
    high = x.astype(jnp.bfloat16)
    return high, (x - high.astype(jnp.float32)).astype(jnp.bfloat16)


def upper_lanes(rows):
    return lax.broadcasted_iota(jnp.int32, (rows, LANES), 1) >= B


def stencil(ref, a, mixers, centre_weight, scale):
    def read(plane, row):
        return ref[pl.ds(a + 2 + plane, SPAN), PAD + row : PAD + row + HALF, :].reshape(SPAN * HALF, LANES)

    here, below, above = read(0, 0), read(0, -1), read(0, 1)
    side = here + jnp.where(upper_lanes(SPAN * HALF), below, above)
    mixed = jnp.dot(
        jnp.concatenate([*halves(here), *halves(side)], axis=1), mixers, preferred_element_type=jnp.float32
    )
    near = read(-1, 0) + read(1, 0)
    far = (read(-2, 0) + read(2, 0)) + (below + above)
    return here, centre_weight * here + scale * (mixed + (far - 16.0 * near))


def over_spans(body):
    def one(i, carry):
        body(i * SPAN)
        return carry

    lax.fori_loop(0, B // SPAN, one, 0)


def clear_edges(ref):
    deep = ref.shape[0]
    zero = jnp.zeros((PAD, LANES), jnp.float32)

    def one(a, carry):
        ref[a, :PAD, :] = zero
        ref[a, PAD + HALF :, :] = zero
        return carry

    lax.fori_loop(0, deep, one, 0, unroll=4)
    if deep == DEEP:
        for a in (0, 1, DEEP - 2, DEEP - 1):
            ref[a] = jnp.zeros((HIGH, LANES), jnp.float32)


def inner_rows(ref):
    lead = (ref.shape[0] - B) // 2
    return ref.at[pl.ds(lead, B), pl.ds(PAD, HALF), :]


def kinetic_kernel(mix, boxes, out, box, result, sem):
    copy = pltpu.make_async_copy(boxes.at[:, 0], inner_rows(box), sem)
    copy.start()
    clear_edges(box)
    copy.wait()
    mixers = mix[...]

    def body(a):
        _, found = stencil(box, a, mixers, -0.5 * 7.5, -0.5 / 12.0)
        result[pl.ds(a, SPAN)] = found.reshape(SPAN, HALF, LANES)

    over_spans(body)
    back = pltpu.make_async_copy(result, out, sem)
    back.start()
    back.wait()


def shifted_plane(ref, a, offset, upper, cell):
    lead = (ref.shape[0] - B) // 2
    o0, o1, o2 = offset
    half = lax.shift_right_arithmetic(o1, 1)
    odd = o1 & 1
    source = a + o0
    inside = jnp.logical_and(source >= 0, source < B)
    source = jnp.clip(source, 0, B - 1) + lead
    low = ref[source, pl.ds(PAD + half, HALF), :]
    high = ref[source, pl.ds(PAD + half + odd, HALF), :]
    mixed = jnp.where(upper == (odd == 1), low, high)
    turned = pltpu.roll(mixed, (2 * LANES - o2 - B * odd) & (LANES - 1), 1)
    reached = cell + o2
    keep = jnp.logical_and(jnp.logical_and(reached >= 0, reached < B), inside)
    return jnp.where(keep, turned, 0.0)


def pairs_kernel(dist, offs, mix, boxes, peers, order, kept, sent,
                 own, near, rho, work_a, work_b, moved, force, sems, out_sem):
    own_copy = pltpu.make_async_copy(boxes.at[:, 0], own, sems.at[3])
    own_copy.start()
    sources = {1: peers.at[:, 0], 2: boxes.at[:, 1], 3: peers.at[:, 1], 4: boxes.at[:, 2]}
    ends = {0: kept.at[:, 0], 1: sent.at[:, 0], 2: kept.at[:, 1], 3: sent.at[:, 1], 4: kept.at[:, 2]}

    def fetch(source, q):
        pltpu.make_async_copy(source, inner_rows(near.at[q]), sems.at[q]).start()

    def deliver(which, sem):
        pltpu.make_async_copy(force.at[which], ends[which], sem).start()

    for q in range(3):
        for far, source in sources.items():
            pl.when(dist[q] == far)(functools.partial(fetch, source, q))
    absent = 10 - dist[0] - dist[1] - dist[2]

    def blank(a, carry):
        force[absent, a] = jnp.zeros((HALF, LANES), jnp.float32)
        force[0, a] = jnp.zeros((HALF, LANES), jnp.float32)
        return carry

    lax.fori_loop(0, B, blank, 0, unroll=4)
    for which in sources:
        pl.when(absent == which)(functools.partial(deliver, which, out_sem.at[3]))
    for q in range(3):
        clear_edges(near.at[q])
    for buffer in (rho, work_a, work_b):
        clear_edges(buffer)
    cell = lax.broadcasted_iota(jnp.int32, (HALF, LANES), 1) & (B - 1)
    upper = upper_lanes(HALF)
    mixers = mix[...]
    centre, radius, poly = sweep_polynomial()
    poly = [exact_share * c for c in poly]
    centre_weight = (7.5 - centre) / radius
    scale = 1.0 / 12.0 / radius
    rows = pl.ds(PAD, HALF)
    own_copy.wait()

    def pair(q, carry):
        offset = (offs[3 * q], offs[3 * q + 1], offs[3 * q + 2])
        back = tuple(-o for o in offset)
        partner = near.at[q]
        target = dist[q]
        pltpu.make_async_copy(boxes.at[:, 0], inner_rows(partner), sems.at[q]).wait()

        def overlap(a, carry):
            there = shifted_plane(partner, a, offset, upper, cell)
            moved[a] = there
            rho[a + 2, rows, :] = own[a] * there
            return carry

        def sweep_one(a):
            here, found = stencil(rho, a, mixers, poly[3] * centre_weight, poly[3] * scale)
            work_a[pl.ds(a + 2, SPAN), rows, :] = (found + poly[2] * here).reshape(SPAN, HALF, LANES)

        def sweep_two(a):
            _, found = stencil(work_a, a, mixers, centre_weight, scale)
            found = found.reshape(SPAN, HALF, LANES)
            work_b[pl.ds(a + 2, SPAN), rows, :] = found + poly[1] * rho[pl.ds(a + 2, SPAN), rows, :]

        def sweep_three(a):
            _, found = stencil(work_b, a, mixers, centre_weight, scale)
            here = pl.ds(a, SPAN)
            inner = pl.ds(a + 2, SPAN)
            found = found.reshape(SPAN, HALF, LANES) + poly[0] * rho[inner, rows, :]
            force[0, here] += found * moved[here]
            work_a[inner, rows, :] = found * own[here]

        def give(a, carry):
            force[target, a] = shifted_plane(work_a, a, back, upper, cell)
            return carry

        lax.fori_loop(0, B, overlap, 0, unroll=16)
        over_spans(sweep_one)
        over_spans(sweep_two)
        over_spans(sweep_three)
        lax.fori_loop(0, B, give, 0, unroll=16)
        for which in sources:
            pl.when(target == which)(functools.partial(deliver, which, out_sem.at[q]))
        return carry

    lax.fori_loop(0, 3, pair, 0)
    deliver(0, out_sem.at[4])
    for k in range(5):
        pltpu.make_async_copy(force.at[0], ends[0], out_sem.at[k]).wait()


F32 = jnp.float32
ANY = pl.BlockSpec(memory_space=pl.ANY)
WHOLE = pl.BlockSpec(memory_space=pltpu.VMEM)
SCALARS = pl.BlockSpec(memory_space=pltpu.SMEM)


def kinetic_of(boxes):
    return pl.pallas_call(
        kinetic_kernel,
        out_shape=jax.ShapeDtypeStruct((B, HALF, LANES), F32),
        in_specs=[WHOLE, ANY],
        out_specs=ANY,
        scratch_shapes=[
            pltpu.VMEM((DEEP, HIGH, LANES), F32),
            pltpu.VMEM((B, HALF, LANES), F32),
            pltpu.SemaphoreType.DMA,
        ],
        cost_estimate=pl.CostEstimate(flops=20 * B**3, transcendentals=0, bytes_accessed=8 * B**3),
        name="kinetic",
    )(lane_mixers(), boxes)


def pair_forces(dist, offs, boxes, peers, order):
    padded = pltpu.VMEM((DEEP, HIGH, LANES), F32)
    return pl.pallas_call(
        pairs_kernel,
        out_shape=[
            jax.ShapeDtypeStruct((B, 3, HALF, LANES), F32),
            jax.ShapeDtypeStruct((B, 2, HALF, LANES), F32),
        ],
        in_specs=[SCALARS, SCALARS, WHOLE, ANY, ANY, ANY],
        out_specs=[ANY, ANY],
        scratch_shapes=[
            pltpu.VMEM((B, HALF, LANES), F32),
            pltpu.VMEM((3, B, HIGH, LANES), F32),
            padded,
            padded,
            padded,
            pltpu.VMEM((B, HALF, LANES), F32),
            pltpu.VMEM((5, B, HALF, LANES), F32),
            pltpu.SemaphoreType.DMA((4,)),
            pltpu.SemaphoreType.DMA((5,)),
        ],
        cost_estimate=pl.CostEstimate(flops=300 * B**3, transcendentals=0, bytes_accessed=40 * B**3),
        name="pairs",
    )(dist, offs, lane_mixers(), boxes, peers, order)


def from_behind(array, axis, by):
    count = lax.axis_size(axis)
    return lax.ppermute(array, axis, [(i, (i + by) % count) for i in range(count)])


def core_swap(array):
    count = lax.axis_size("grid")
    return lax.ppermute(array, "grid", [(i, i ^ 1) for i in range(count)])


def local(orbitals, previous, potential, partners, offsets):
    slabs = lax.axis_size("grid")
    total = lax.axis_size("orb") * slabs
    place = lax.axis_index(("orb", "grid"))
    core = place & 1
    dist = jnp.remainder(partners[0] - place, total)
    offs = offsets.reshape(-1)

    upper = from_behind(orbitals[:AHEAD], "orb", -1)
    longer = jnp.concatenate([orbitals, upper], axis=0)
    windows = jnp.stack([longer[:slabs], longer[2 : 2 + slabs], longer[4 : 4 + slabs]], axis=1)
    boxes = lax.all_to_all(windows, "grid", split_axis=0, concat_axis=0, tiled=True)
    offered = lax.dynamic_slice_in_dim(boxes, 1 - core, 2, axis=1)
    peers = core_swap(offered)
    own_kinetic = kinetic_of(boxes)
    kinetic = lax.all_to_all(own_kinetic, "grid", split_axis=0, concat_axis=0, tiled=True)
    kept, sent = pair_forces(dist, offs, boxes, peers, own_kinetic)
    given = core_swap(sent)
    even = core == 0
    zero = jnp.zeros_like(given[:, 0])
    summed = kept + jnp.stack(
        [
            jnp.where(even, zero, given[:, 0]),
            jnp.where(even, given[:, 0], given[:, 1]),
            jnp.where(even, given[:, 1], zero),
        ],
        axis=1,
    )
    summed, kinetic = lax.optimization_barrier((summed, kinetic))
    returned = lax.all_to_all(summed, "grid", split_axis=0, concat_axis=0, tiled=True)
    own, two, four = returned[:, 0], returned[:, 1], returned[:, 2]
    spill = four[slabs - 4 :] + jnp.pad(two[slabs - 2 :], ((0, 2), (0, 0), (0, 0)))
    spill = from_behind(spill, "orb", 1)
    exchange_force = own + jnp.concatenate(
        [spill[:2], spill[2:] + two[:2], two[2 : slabs - 2] + four[: slabs - 4]], axis=0
    )
    advanced = (
        2.0 * orbitals
        - previous
        + verlet_factor * (kinetic + exchange_force - potential * orbitals)
    )
    return advanced, exchange_force


def solution(mesh):
    rows = P("orb", "grid", None)
    return jax.shard_map(
        local,
        mesh=mesh,
        in_specs=(rows, rows, rows, P(("orb", "grid"), None), P(("orb", "grid"), None, None)),
        out_specs=(rows, rows),
        check_vma=False,
    )
```

time: 282 us -> 242 us (0.86)
  blocking collectives: 0 us -> 79.2 us
  waiting for transfers between devices: 176 us -> 105 us
  Pallas kernels: 59.1 us -> 20.7 us
  other arithmetic: 12.7 us -> 7.25 us
  starting transfers between devices: 27.3 us -> 22.3 us
    all_to_all x0 -> x1, blocking collectives: none -> 79.2 us  [local(): lax.all_to_all(summed, 'grid', split_axis=0, concat_axis=0, tiled=True)]
    all_to_all x2 -> x1, waiting for transfers between devices: 90.5 us -> 26 us  [local(): lax.all_to_all(own_kinetic, 'grid', split_axis=0, concat_axis=0, tiled=True)]
    pallas_call x1, Pallas kernels: 53.3 us -> 16.6 us  [pair_forces(): pl.pallas_call(pairs_kernel, out_shape=[jax.ShapeDtypeStruct((B, 3, HALF,...]
    ppermute x2, waiting for transfers between devices: 7.72 us -> 0.01 us  [core_swap(): return lax.ppermute(array, 'grid', [(i, i ^ 1) for i in range(count)])]
    all_to_all x2 -> x1, starting transfers between devices: 11.1 us -> 5.59 us  [local(): lax.all_to_all(own_kinetic, 'grid', split_axis=0, concat_axis=0, tiled=True)]
  transfers between devices with their start and end apart: 7 -> 6, of which waited for: 7 -> 4; matrix products, arithmetic and copies ran while one was open for 1% -> 2% of each run, Pallas kernels for 2% -> 2%
where the time goes in v2:
time: 242 us; the launch traced here: 241 us
  waiting for transfers between devices  105 us (43%)
  blocking collectives  79.2 us (33%)
  starting transfers between devices  22.3 us (9%)
  Pallas kernels  20.7 us (9%)
  other arithmetic  7.25 us (3%)
  local copies, waits for them, and re-layouts  6.21 us (3%)
    all_to_all x1, blocking collectives, local(): lax.all_to_all(summed, 'grid', split_axis=0, concat_axis=0, tiled=True)  79.2 us
    all_to_all x1, waiting for transfers between devices, local(): lax.all_to_all(windows, 'grid', split_axis=0, concat_axis=0, tiled=True)  73.7 us
    all_to_all x1, waiting for transfers between devices, local(): lax.all_to_all(own_kinetic, 'grid', split_axis=0, concat_axis=0, tiled=True)  26 us
    pallas_call x1, Pallas kernels, pair_forces(): pl.pallas_call(pairs_kernel, out_shape=[jax.ShapeDtypeStruct((B, 3, HALF,...  16.6 us
    all_to_all x1, starting transfers between devices, local(): lax.all_to_all(windows, 'grid', split_axis=0, concat_axis=0, tiled=True)  12 us
    all_to_all x1, starting transfers between devices, local(): lax.all_to_all(own_kinetic, 'grid', split_axis=0, concat_axis=0, tiled=True)  5.59 us
    ppermute x2, waiting for transfers between devices, from_behind(): lax.ppermute(array, axis, [(i, (i + by) % count) for i in range(count)])  5.22 us
  transfers between devices with their start and end apart: 6, of which 4 were waited for; matrix products, arithmetic and copies ran while one was open for 2% of the time, Pallas kernels for 2%

profile of v2, /device:TPU:2, one launch (start us, length us, event | category | flops | bytes accessed | tf_op | source)
XLA Modules:
  0.0 241.4 jit_solution(4136686391431557898)
XLA Ops:
  0.6 0.8 slice.59
  1.5 3.0 %collective-permute-start = (f32[4,32,128]{2,1,0:T(8,128)S(1)}, f32[4,32,128]{2,1,0:T(8,128)S(1)}, u32[]{:S(2)}, u32[]{:S(2)}) collective-permute-start(f32[4,32,128]{2,1,0:T(8,128)S(1)} %slice.59), channel_id=1, source_target_pairs={{0,192},{64,0},{128,64},{192,128},{1,193},{65,1},{129,65},{193,129... | collective-permute-start | bytes 196616 | tf_op jit(solution)/shard_map/ppermute | solution.py:284
  4.5 1.3 constant_dynamic-update-slice_fusion.1
  5.8 0.6 collective-permute-done
  6.4 0.2 slice_bitcast_fusion.2
  6.7 0.0 copy-done.1
  6.7 2.0 pad_maximum_fusion
  8.6 12.0 %all-to-all-start = ((f32[64,3,32,128]{3,2,1,0:T(8,128)}), f32[64,3,32,128]{3,2,1,0:T(8,128)S(1)}, u32[]{:S(2)}, u32[]{:S(2)}) async-start(f32[64,3,32,128]{3,2,1,0:T(8,128)} %pad_maximum_fusion), calls=%async_computation | async-start | bytes 6291456 | tf_op jit(solution)/shard_map/all_to_all | solution.py:303
  20.7 0.0 copy-start.6
  20.7 0.0 copy-start.7
  20.7 73.7 %all-to-all-done.boxes = f32[64,3,32,128]{3,2,1,0:T(8,128)S(1)} async-done(((f32[64,3,32,128]{3,2,1,0:T(8,128)}), f32[64,3,32,128]{3,2,1,0:T(8,128)S(1)}, u32[]{:S(2)}, u32[]{:S(2)}) %all-to-all-start) | async-done | bytes 3145760 | tf_op jit(solution)/shard_map/all_to_all | solution.py:303
  94.4 1.8 constant_dynamic-slice_fusion
  96.1 0.0 collective-permute-start.1
  96.1 0.0 copy-done.6
  96.2 0.6 reshape.15.offs
  96.8 0.5 and_select_fusion.dist
  97.3 0.0 copy-done
  97.3 4.0 %kinetic.1.order = f32[64,32,128]{2,1,0:T(8,128)} custom-call(bf16[512,128]{1,0:T(8,128)(2,1)} %constant.41.clone.mix, f32[64,3,32,128]{3,2,1,0:T(8,128)} %copy-done), custom_call_target="tpu_custom_call" | custom-call | flops 5242880 | bytes 2097152 | tf_op jit(solution)/shard_map/kinetic/pallas_call | solution.py:241
  101.4 0.0 collective-permute-done.1.peers
  101.4 16.6 %pairs.1 = (f32[64,3,32,128]{3,2,1,0:T(8,128)}, f32[64,2,32,128]{3,2,1,0:T(8,128)}) custom-call(s32[3]{0:T(128)} %and_select_fusion.dist, s32[9]{0:T(128)} %reshape.15.offs, bf16[512,128]{1,0:T(8,128)(2,1)} %constant.41.clone.mix, f32[64,3,32,128]{3,2,1,0:T(8,128)} %copy-done, f32[64,2,32,128]{3,2,1,0:T(8,128)} %collective-permute-done.1.peers, ...), custom_call_target="tpu_custom_call" | custom-call | flops 78643200 | bytes 10485760 | tf_op jit(solution)/shard_map/pairs/pallas_call | solution.py:258
  118.0 0.7 collective-permute-start.2
  118.7 5.6 %all-to-all-start.1 = ((f32[64,32,128]{2,1,0:T(8,128)}), f32[64,32,128]{2,1,0:T(8,128)}, u32[]{:S(2)}, u32[]{:S(2)}) async-start(f32[64,32,128]{2,1,0:T(8,128)} %kinetic.1.order), calls=%async_computation.1 | async-start | bytes 2097152 | tf_op jit(solution)/shard_map/all_to_all | solution.py:307
  124.3 0.0 collective-permute-done.2
  124.3 0.5 slice_select_fusion.2
  124.8 1.4 copy-done.3
  126.2 0.8 maximum_add_fusion
  126.9 26.0 %all-to-all-done.1 = f32[64,32,128]{2,1,0:T(8,128)} async-done(((f32[64,32,128]{2,1,0:T(8,128)}), f32[64,32,128]{2,1,0:T(8,128)}, u32[]{:S(2)}, u32[]{:S(2)}) %all-to-all-start.1) | async-done | bytes 1048608 | tf_op jit(solution)/shard_map/all_to_all | solution.py:307
  153.0 79.2 %all_to_all.15 = f32[64,3,32,128]{3,2,1,0:T(8,128)S(1)} all-to-all(f32[64,3,32,128]{3,2,1,0:T(8,128)S(1)} %maximum_add_fusion), channel_id=1, replica_groups=mesh['orb'=4,'grid'=64] {'grid'}, dimensions={0} | all-to-all | bytes 6291456 | tf_op jit(solution)/shard_map/all_to_all | solution.py:321
  232.2 1.0 collective-permute-start.3
  233.2 0.2 fusion.1
  233.4 4.6 %collective-permute-done.3 = f32[4,32,128]{2,1,0:T(8,128)S(1)} collective-permute-done((f32[4,32,128]{2,1,0:T(8,128)S(1)}, f32[4,32,128]{2,1,0:T(8,128)S(1)}, u32[]{:S(2)}, u32[]{:S(2)}) %collective-permute-start.3) | collective-permute-done | bytes 65568 | tf_op jit(solution)/shard_map/ppermute | solution.py:284
  238.1 3.3 %multiply_add_fusion = (f32[64,32,128]{2,1,0:T(8,128)}, f32[64,32,128]{2,1,0:T(8,128)}) fusion(f32[64,32,128]{2,1,0:T(8,128)S(1)} %copy-done.4, f32[64,32,128]{2,1,0:T(8,128)S(1)} %copy-done.2, f32[64,32,128]{2,1,0:T(8,128)} %all-to-all-done.1, f32[64,32,128]{2,1,0:T(8,128)S(1)} %copy-done.5, f32[60,32,128]{2,1,0:T(8,128)S(1)} %fusion.1, ...), kind=kLoop, calls=%fused_computation.6 | loop fusion | flops 2621440 | bytes 8388608 | tf_op jit(solution)/shard_map/add | solution.py:329
  (15 shorter events, 0.1 us)
Async XLA Ops:
  1.5 5.2 %copy-start.1 = (f32[64,32,128]{2,1,0:T(8,128)S(1)}, f32[64,32,128]{2,1,0:T(8,128)}, u32[]{:S(2)}) copy-start(f32[64,32,128]{2,1,0:T(8,128)} %param.7) | copy-start | bytes 3145732
  1.5 4.9 %collective-permute-start = (f32[4,32,128]{2,1,0:T(8,128)S(1)}, f32[4,32,128]{2,1,0:T(8,128)S(1)}, u32[]{:S(2)}, u32[]{:S(2)}) collective-permute-start(f32[4,32,128]{2,1,0:T(8,128)S(1)} %slice.59), channel_id=1, source_target_pairs={{0,192},{64,0},{128,64},{192,128},{1,193},{65,1},{129,65},{193,129... | collective-permute-start | bytes 196616 | tf_op jit(solution)/shard_map/ppermute | solution.py:284
  8.6 85.7 %all-to-all-start = ((f32[64,3,32,128]{3,2,1,0:T(8,128)}), f32[64,3,32,128]{3,2,1,0:T(8,128)S(1)}, u32[]{:S(2)}, u32[]{:S(2)}) async-start(f32[64,3,32,128]{3,2,1,0:T(8,128)} %pad_maximum_fusion), calls=%async_computation | async-start | bytes 6291456 | tf_op jit(solution)/shard_map/all_to_all | solution.py:303
  20.7 75.5 %copy-start.6 = (s32[1,3,3]{2,0,1:T(1,128)S(1)}, s32[1,3,3]{2,0,1:T(1,128)}, u32[]{:S(2)}) copy-start(s32[1,3,3]{2,0,1:T(1,128)} %param.11) | copy-start | bytes 112
  20.7 76.1 %copy-start.7 = (s32[1,3]{1,0:T(1,128)S(1)}, s32[1,3]{1,0:T(1,128)}, u32[]{:S(2)}) copy-start(s32[1,3]{1,0:T(1,128)} %param.10) | copy-start | bytes 40
  94.4 2.9 %copy-start = (f32[64,3,32,128]{3,2,1,0:T(8,128)}, f32[64,3,32,128]{3,2,1,0:T(8,128)S(1)}, u32[]{:S(2)}) copy-start(f32[64,3,32,128]{3,2,1,0:T(8,128)S(1)} %all-to-all-done.boxes) | copy-start | bytes 9437188
  96.1 5.2 %collective-permute-start.1 = (f32[64,2,32,128]{3,2,1,0:T(8,128)}, f32[64,2,32,128]{3,2,1,0:T(8,128)}, u32[]{:S(2)}, u32[]{:S(2)}) collective-permute-start(f32[64,2,32,128]{3,2,1,0:T(8,128)} %constant_dynamic-slice_fusion), channel_id=1, source_target_pairs={{0,1},{1,0},{2,3},{3,2},{4,5},{5,4},{6,7},{7,6},{8,9},{9,8},{10,11... | collective-permute-start | bytes 6291464 | tf_op jit(solution)/shard_map/ppermute | solution.py:289
  118.0 6.3 %collective-permute-start.2 = (f32[64,2,32,128]{3,2,1,0:T(8,128)}, f32[64,2,32,128]{3,2,1,0:T(8,128)S(1)}, u32[]{:S(2)}, u32[]{:S(2)}) collective-permute-start(f32[64,2,32,128]{3,2,1,0:T(8,128)} %get-tuple-element.7), channel_id=1, source_target_pairs={{0,1},{1,0},{2,3},{3,2},{4,5},{5,4},{6,7},{7,6},{8,9},{9,8},{10,11... | collective-permute-start | bytes 6291464 | tf_op jit(solution)/shard_map/ppermute | solution.py:289
  118.7 34.3 %all-to-all-start.1 = ((f32[64,32,128]{2,1,0:T(8,128)}), f32[64,32,128]{2,1,0:T(8,128)}, u32[]{:S(2)}, u32[]{:S(2)}) async-start(f32[64,32,128]{2,1,0:T(8,128)} %kinetic.1.order), calls=%async_computation.1 | async-start | bytes 2097152 | tf_op jit(solution)/shard_map/all_to_all | solution.py:307
  124.3 1.9 copy-start.3
  232.1 5.9 %copy-start.2 = (f32[64,32,128]{2,1,0:T(8,128)S(1)}, f32[64,32,128]{2,1,0:T(8,128)}, u32[]{:S(2)}) copy-start(f32[64,32,128]{2,1,0:T(8,128)} %param.7) | copy-start | bytes 3145732
  232.1 5.9 %copy-start.4 = (f32[64,32,128]{2,1,0:T(8,128)S(1)}, f32[64,32,128]{2,1,0:T(8,128)}, u32[]{:S(2)}) copy-start(f32[64,32,128]{2,1,0:T(8,128)} %param.9) | copy-start | bytes 3145732
  232.1 5.9 %copy-start.5 = (f32[64,32,128]{2,1,0:T(8,128)S(1)}, f32[64,32,128]{2,1,0:T(8,128)}, u32[]{:S(2)}) copy-start(f32[64,32,128]{2,1,0:T(8,128)} %param.8) | copy-start | bytes 3145732
  232.2 5.9 %collective-permute-start.3 = (f32[4,32,128]{2,1,0:T(8,128)S(1)}, f32[4,32,128]{2,1,0:T(8,128)S(1)}, u32[]{:S(2)}, u32[]{:S(2)}) collective-permute-start(f32[4,32,128]{2,1,0:T(8,128)S(1)} %fusion.2), channel_id=1, source_target_pairs={{0,64},{64,128},{128,192},{192,0},{1,65},{65,129},{129,193},{193,1... | collective-permute-start | bytes 196616 | tf_op jit(solution)/shard_map/ppermute | solution.py:284

commit v3 on v2

--- a/solution.py
+++ b/solution.py
@@ -18,6 +18,7 @@
 HIGH = HALF + 2 * PAD
 DEEP = B + 4
 SPAN = 32
+GROUP = 8
 
 coulomb_factor = 4.0 * np.pi
 exact_share = 0.25
@@ -108,21 +109,34 @@
     return ref.at[pl.ds(lead, B), pl.ds(PAD, HALF), :]
 
 
-def kinetic_kernel(mix, boxes, out, box, result, sem):
-    copy = pltpu.make_async_copy(boxes.at[:, 0], inner_rows(box), sem)
-    copy.start()
-    clear_edges(box)
-    copy.wait()
-    mixers = mix[...]
-
-    def body(a):
-        _, found = stencil(box, a, mixers, -0.5 * 7.5, -0.5 / 12.0)
-        result[pl.ds(a, SPAN)] = found.reshape(SPAN, HALF, LANES)
-
-    over_spans(body)
-    back = pltpu.make_async_copy(result, out, sem)
-    back.start()
-    back.wait()
+def slab_kernel(place, mix, own, low, high, peer, peer_low, peer_high, previous, potential, out, box):
+    slab = place[0]
+    core = slab & 1
+    rows = pl.ds(PAD, HALF)
+
+    @pl.when(pl.program_id(0) == 0)
+    def _():
+        clear_edges(box)
+
+    here = own[...]
+    box[:, rows, :] = here
+    zero = jnp.zeros_like(here)
+    below = jnp.where(slab > 1, low[...], zero)
+    above = jnp.where(slab < place[1] - 2, high[...], zero)
+    edge = jnp.where(core == 0, peer_low[...], peer_high[...])
+    held = jnp.logical_or(jnp.logical_and(core == 0, slab > 1), jnp.logical_and(core == 1, slab < place[1] - 2))
+    near = peer[...] + jnp.where(held, edge, zero)
+    far = below + above
+    flat = here.reshape(GROUP * HALF, LANES)
+    lower = box[:, PAD - 1 : PAD - 1 + HALF, :].reshape(GROUP * HALF, LANES)
+    upper = box[:, PAD + 1 : PAD + 1 + HALF, :].reshape(GROUP * HALF, LANES)
+    side = flat + jnp.where(upper_lanes(GROUP * HALF), lower, upper)
+    mixed = jnp.dot(
+        jnp.concatenate([*halves(flat), *halves(side)], axis=1), mix[...], preferred_element_type=jnp.float32
+    )
+    mixed = (mixed + (lower + upper)).reshape(GROUP, HALF, LANES)
+    kinetic = -3.75 * here - (mixed + (far - 16.0 * near)) / 24.0
+    out[...] = 2.0 * here - previous[...] + verlet_factor * (kinetic - potential[...] * here)
 
 
 def shifted_plane(ref, a, offset, upper, cell):
@@ -142,11 +156,13 @@
     return jnp.where(keep, turned, 0.0)
 
 
-def pairs_kernel(dist, offs, mix, boxes, peers, order, kept, sent,
+def pairs_kernel(place, partners, offsets, mix, boxes, peers, kept, sent,
                  own, near, rho, work_a, work_b, moved, force, sems, out_sem):
+    core = place[0] & 1
+    dist = [jnp.remainder(partners[0, q] - place[0] + place[1], place[1]) for q in range(3)]
     own_copy = pltpu.make_async_copy(boxes.at[:, 0], own, sems.at[3])
     own_copy.start()
-    sources = {1: peers.at[:, 0], 2: boxes.at[:, 1], 3: peers.at[:, 1], 4: boxes.at[:, 2]}
+    sources = {1: peers.at[:, core], 2: boxes.at[:, 1], 3: peers.at[:, 1 + core], 4: boxes.at[:, 2]}
     ends = {0: kept.at[:, 0], 1: sent.at[:, 0], 2: kept.at[:, 1], 3: sent.at[:, 1], 4: kept.at[:, 2]}
 
     def fetch(source, q):
@@ -183,10 +199,10 @@
     own_copy.wait()
 
     def pair(q, carry):
-        offset = (offs[3 * q], offs[3 * q + 1], offs[3 * q + 2])
+        offset = (offsets[0, q, 0], offsets[0, q, 1], offsets[0, q, 2])
         back = tuple(-o for o in offset)
         partner = near.at[q]
-        target = dist[q]
+        target = jnp.where(q == 0, dist[0], jnp.where(q == 1, dist[1], dist[2]))
         pltpu.make_async_copy(boxes.at[:, 0], inner_rows(partner), sems.at[q]).wait()
 
         def overlap(a, carry):
@@ -237,23 +253,21 @@
 SCALARS = pl.BlockSpec(memory_space=pltpu.SMEM)
 
 
-def kinetic_of(boxes):
+def slab_terms(place, arrays):
+    block = pl.BlockSpec((GROUP, HALF, LANES), lambda i: (i, 0, 0))
     return pl.pallas_call(
-        kinetic_kernel,
-        out_shape=jax.ShapeDtypeStruct((B, HALF, LANES), F32),
-        in_specs=[WHOLE, ANY],
-        out_specs=ANY,
-        scratch_shapes=[
-            pltpu.VMEM((DEEP, HIGH, LANES), F32),
-            pltpu.VMEM((B, HALF, LANES), F32),
-            pltpu.SemaphoreType.DMA,
-        ],
-        cost_estimate=pl.CostEstimate(flops=20 * B**3, transcendentals=0, bytes_accessed=8 * B**3),
-        name="kinetic",
-    )(lane_mixers(), boxes)
-
-
-def pair_forces(dist, offs, boxes, peers, order):
+        slab_kernel,
+        grid=(arrays[0].shape[0] // GROUP,),
+        out_shape=jax.ShapeDtypeStruct(arrays[0].shape, F32),
+        in_specs=[SCALARS, WHOLE] + [block] * len(arrays),
+        out_specs=block,
+        scratch_shapes=[pltpu.VMEM((GROUP, HIGH, LANES), F32)],
+        cost_estimate=pl.CostEstimate(flops=20 * B**3, transcendentals=0, bytes_accessed=36 * B**3),
+        name="slab",
+    )(place, lane_mixers(), *arrays)
+
+
+def pair_forces(place, partners, offsets, boxes, peers):
     padded = pltpu.VMEM((DEEP, HIGH, LANES), F32)
     return pl.pallas_call(
         pairs_kernel,
@@ -261,7 +275,7 @@
             jax.ShapeDtypeStruct((B, 3, HALF, LANES), F32),
             jax.ShapeDtypeStruct((B, 2, HALF, LANES), F32),
         ],
-        in_specs=[SCALARS, SCALARS, WHOLE, ANY, ANY, ANY],
+        in_specs=[SCALARS, SCALARS, SCALARS, WHOLE, ANY, ANY],
         out_specs=[ANY, ANY],
         scratch_shapes=[
             pltpu.VMEM((B, HALF, LANES), F32),
@@ -276,7 +290,7 @@
         ],
         cost_estimate=pl.CostEstimate(flops=300 * B**3, transcendentals=0, bytes_accessed=40 * B**3),
         name="pairs",
-    )(dist, offs, lane_mixers(), boxes, peers, order)
+    )(place, partners, offsets, lane_mixers(), boxes, peers)
 
 
 def from_behind(array, axis, by):
@@ -292,22 +306,21 @@
 def local(orbitals, previous, potential, partners, offsets):
     slabs = lax.axis_size("grid")
     total = lax.axis_size("orb") * slabs
-    place = lax.axis_index(("orb", "grid"))
-    core = place & 1
-    dist = jnp.remainder(partners[0] - place, total)
-    offs = offsets.reshape(-1)
+    index = lax.axis_index("grid")
+    even = (index & 1) == 0
+    place = jnp.stack([lax.axis_index(("orb", "grid")), jnp.int32(total)])
+    slab = jnp.stack([index, jnp.int32(slabs)])
 
     upper = from_behind(orbitals[:AHEAD], "orb", -1)
     longer = jnp.concatenate([orbitals, upper], axis=0)
     windows = jnp.stack([longer[:slabs], longer[2 : 2 + slabs], longer[4 : 4 + slabs]], axis=1)
     boxes = lax.all_to_all(windows, "grid", split_axis=0, concat_axis=0, tiled=True)
-    offered = lax.dynamic_slice_in_dim(boxes, 1 - core, 2, axis=1)
-    peers = core_swap(offered)
-    own_kinetic = kinetic_of(boxes)
-    kinetic = lax.all_to_all(own_kinetic, "grid", split_axis=0, concat_axis=0, tiled=True)
-    kept, sent = pair_forces(dist, offs, boxes, peers, own_kinetic)
+    peers = core_swap(boxes)
+    source, _ = lax.optimization_barrier((orbitals, boxes))
+    low = from_behind(source, "grid", 2)
+    high = from_behind(source, "grid", -2)
+    kept, sent = pair_forces(place, partners, offsets, boxes, peers)
     given = core_swap(sent)
-    even = core == 0
     zero = jnp.zeros_like(given[:, 0])
     summed = kept + jnp.stack(
         [
@@ -317,20 +330,17 @@
         ],
         axis=1,
     )
-    summed, kinetic = lax.optimization_barrier((summed, kinetic))
+    summed, low, high = lax.optimization_barrier((summed, low, high))
     returned = lax.all_to_all(summed, "grid", split_axis=0, concat_axis=0, tiled=True)
+    sides = [core_swap(array) for array in (source, low, high)]
+    base = slab_terms(slab, [orbitals, low, high, *sides, previous, potential])
     own, two, four = returned[:, 0], returned[:, 1], returned[:, 2]
     spill = four[slabs - 4 :] + jnp.pad(two[slabs - 2 :], ((0, 2), (0, 0), (0, 0)))
     spill = from_behind(spill, "orb", 1)
     exchange_force = own + jnp.concatenate(
         [spill[:2], spill[2:] + two[:2], two[2 : slabs - 2] + four[: slabs - 4]], axis=0
     )
-    advanced = (
-        2.0 * orbitals
-        - previous
-        + verlet_factor * (kinetic + exchange_force - potential * orbitals)
-    )
-    return advanced, exchange_force
+    return base + verlet_factor * exchange_force, exchange_force
 
 
 def solution(mesh):

time: 242 us -> 234 us (0.967)
  waiting for transfers between devices: 105 us -> 94.7 us
  blocking collectives: 79.2 us -> 85.5 us
  starting transfers between devices: 22.3 us -> 16.6 us
  Pallas kernels: 20.7 us -> 24.3 us
  local copies, waits for them, and re-layouts: 6.21 us -> 3.04 us
    all_to_all x2 -> x1, waiting for transfers between devices: 99.7 us -> 59.9 us  [local(): lax.all_to_all(summed, 'grid', split_axis=0, concat_axis=0, tiled=True)]
    ppermute x2 -> x4, waiting for transfers between devices: 5.22 us -> 23.5 us  [from_behind(): lax.ppermute(array, axis, [(i, (i + by) % count) for i in range(count)])]
    ppermute x2 -> x5, waiting for transfers between devices: 0.01 us -> 11.4 us  [core_swap(): return lax.ppermute(array, 'grid', [(i, i ^ 1) for i in range(count)])]
    all_to_all x2 -> x1, starting transfers between devices: 17.6 us -> 9.62 us  [local(): lax.all_to_all(summed, 'grid', split_axis=0, concat_axis=0, tiled=True)]
    all_to_all x1, blocking collectives: 79.2 us -> 85.5 us  [local(): lax.all_to_all(windows, 'grid', split_axis=0, concat_axis=0, tiled=True)]
    pallas_call x1, Pallas kernels: 4.04 us -> 7.73 us  [slab_terms(): pl.pallas_call(slab_kernel, grid=(arrays[0].shape[0] // GROUP,), out_shap...]
    ppermute x2 -> x4, starting transfers between devices: 4.06 us -> 6.04 us  [from_behind(): lax.ppermute(array, axis, [(i, (i + by) % count) for i in range(count)])]
  transfers between devices with their start and end apart: 6 -> 10, of which waited for: 4 -> 10; matrix products, arithmetic and copies ran while one was open for 2% -> 3% of each run, Pallas kernels for 2% -> 3%
where the time goes in v3:
time: 234 us; the launch traced here: 233 us
  waiting for transfers between devices  94.7 us (40%)
  blocking collectives  85.5 us (37%)
  Pallas kernels  24.3 us (10%)
  starting transfers between devices  16.6 us (7%)
  other arithmetic  8.15 us (3%)
  local copies, waits for them, and re-layouts  3.04 us (1%)
    all_to_all x1, blocking collectives, local(): lax.all_to_all(windows, 'grid', split_axis=0, concat_axis=0, tiled=True)  85.5 us
    all_to_all x1, waiting for transfers between devices, local(): lax.all_to_all(summed, 'grid', split_axis=0, concat_axis=0, tiled=True)  59.9 us
    ppermute x4, waiting for transfers between devices, from_behind(): lax.ppermute(array, axis, [(i, (i + by) % count) for i in range(count)])  23.5 us
    pallas_call x1, Pallas kernels, pair_forces(): pl.pallas_call(pairs_kernel, out_shape=[jax.ShapeDtypeStruct((B, 3, HALF,...  16.6 us
    ppermute x5, waiting for transfers between devices, core_swap(): return lax.ppermute(array, 'grid', [(i, i ^ 1) for i in range(count)])  11.4 us
    all_to_all x1, starting transfers between devices, local(): lax.all_to_all(summed, 'grid', split_axis=0, concat_axis=0, tiled=True)  9.62 us
    pallas_call x1, Pallas kernels, slab_terms(): pl.pallas_call(slab_kernel, grid=(arrays[0].shape[0] // GROUP,), out_shap...  7.73 us
    ppermute x4, starting transfers between devices, from_behind(): lax.ppermute(array, axis, [(i, (i + by) % count) for i in range(count)])  6.04 us
  transfers between devices with their start and end apart: 10, of which 10 were waited for; matrix products, arithmetic and copies ran while one was open for 3% of the time, Pallas kernels for 3%

profile of v3, /device:TPU:2, one launch (start us, length us, event | category | flops | bytes accessed | tf_op | source)
XLA Modules:
  0.0 233.1 jit_solution(10061622304169782028)
XLA Ops:
  0.6 0.8 slice.59
  1.5 3.0 %collective-permute-start = (f32[4,32,128]{2,1,0:T(8,128)S(1)}, f32[4,32,128]{2,1,0:T(8,128)S(1)}, u32[]{:S(2)}, u32[]{:S(2)}) collective-permute-start(f32[4,32,128]{2,1,0:T(8,128)S(1)} %slice.59), channel_id=1, source_target_pairs={{0,192},{64,0},{128,64},{192,128},{1,193},{65,1},{129,65},{193,129... | collective-permute-start | bytes 196616 | tf_op jit(solution)/shard_map/ppermute | solution.py:298
  4.5 1.3 constant_dynamic-update-slice_fusion.1
  5.8 0.6 collective-permute-done
  6.4 0.2 slice_bitcast_fusion.2
  6.7 0.4 pad_maximum_fusion
  7.1 85.5 %all_to_all.10.boxes = f32[64,3,32,128]{3,2,1,0:T(8,128)S(1)} all-to-all(f32[64,3,32,128]{3,2,1,0:T(8,128)S(1)} %pad_maximum_fusion), channel_id=1, replica_groups=mesh['orb'=4,'grid'=64] {'grid'}, dimensions={0} | all-to-all | bytes 6291456 | tf_op jit(solution)/shard_map/all_to_all | solution.py:317
  92.6 0.6 copy.14.offsets
  93.2 0.8 pad_add_fusion.1.place
  94.1 4.3 %collective-permute-done.1.peers = f32[64,3,32,128]{3,2,1,0:T(8,128)} collective-permute-done((f32[64,3,32,128]{3,2,1,0:T(8,128)S(1)}, f32[64,3,32,128]{3,2,1,0:T(8,128)}, u32[]{:S(2)}, u32[]{:S(2)}) %collective-permute-start.1) | collective-permute-done | bytes 3145760 | tf_op jit(solution)/shard_map/ppermute | solution.py:303
  98.4 16.6 %pairs.1 = (f32[64,3,32,128]{3,2,1,0:T(8,128)}, f32[64,2,32,128]{3,2,1,0:T(8,128)}) custom-call(s32[2]{0:T(128)} %pad_add_fusion.1.place, s32[1,3]{1,0:T(1,128)} %partners.1, s32[1,3,3]{2,1,0:T(4,128)} %copy.14.offsets, bf16[512,128]{1,0:T(8,128)(2,1)} %constant.26.clone.mix, f32[64,3,32,128]{3,2,1,0:T(8,128)} %copy-done, ...), custom_call_target="tpu_custom_call" | custom-call | flops 78643200 | bytes 10485760 | tf_op jit(solution)/shard_map/pairs/pallas_call | solution.py:272
  115.0 0.3 collective-permute-start.2
  115.3 1.5 collective-permute-start.3
  116.8 0.6 collective-permute-start.4
  117.3 2.3 collective-permute-done.2
  119.6 2.0 slice_select_fusion.2
  121.6 2.4 %maximum_add_fusion = f32[64,3,32,128]{3,2,1,0:T(8,128)} fusion(f32[64,3,32,128]{3,2,1,0:T(8,128)S(1)} %copy-done.3, f32[64,1,32,128]{3,2,1,0:T(8,128)S(1)} %get-tuple-element.17, f32[64,1,32,128]{3,2,1,0:T(8,128)S(1)} %get-tuple-element.18, f32[64,1,32,128]{3,2,1,0:T(8,128)S(1)} %get-tuple-element.16), kind=kLoop, calls=%fused_computation.1 | loop fusion | flops 2359296 | bytes 9437184 | tf_op jit(solution)/shard_map/add | solution.py:325
  124.0 16.9 %collective-permute-done.3.low = f32[64,32,128]{2,1,0:T(8,128)} collective-permute-done((f32[64,32,128]{2,1,0:T(8,128)}, f32[64,32,128]{2,1,0:T(8,128)}, u32[]{:S(2)}, u32[]{:S(2)}) %collective-permute-start.3) | collective-permute-done | bytes 1048608 | tf_op jit(solution)/shard_map/ppermute | solution.py:298
  141.0 1.2 collective-permute-done.4.high
  142.2 9.6 %all-to-all-start.1 = ((f32[64,3,32,128]{3,2,1,0:T(8,128)}), f32[64,3,32,128]{3,2,1,0:T(8,128)S(1)}, u32[]{:S(2)}, u32[]{:S(2)}) async-start(f32[64,3,32,128]{3,2,1,0:T(8,128)} %maximum_add_fusion), calls=%async_computation.1 | async-start | bytes 6291456 | tf_op jit(solution)/shard_map/all_to_all | solution.py:334
  151.8 0.2 collective-permute-start.5
  152.0 0.4 collective-permute-start.6
  152.5 0.6 pad_add_fusion.place
  153.1 1.8 collective-permute-done.5.peer
  154.9 1.5 collective-permute-done.6.peer_low
  156.4 1.5 collective-permute-done.7.peer_high
  157.9 7.7 %slab.1 = f32[64,32,128]{2,1,0:T(8,128)} custom-call(s32[2]{0:T(128)} %pad_add_fusion.place, bf16[512,128]{1,0:T(8,128)(2,1)} %constant.26.clone.mix, f32[64,32,128]{2,1,0:T(8,128)} %own.1, f32[64,32,128]{2,1,0:T(8,128)} %collective-permute-done.3.low, f32[64,32,128]{2,1,0:T(8,128)} %collective-permute-done.4.high, ...), custom_call_target="tpu_custom_call" | custom-call | flops 5242880 | bytes 9437184 | tf_op jit(solution)/shard_map/slab/pallas_call | solution.py:258
  165.6 59.9 %all-to-all-done.1 = f32[64,3,32,128]{3,2,1,0:T(8,128)S(1)} async-done(((f32[64,3,32,128]{3,2,1,0:T(8,128)}), f32[64,3,32,128]{3,2,1,0:T(8,128)S(1)}, u32[]{:S(2)}, u32[]{:S(2)}) %all-to-all-start.1) | async-done | bytes 3145760 | tf_op jit(solution)/shard_map/all_to_all | solution.py:334
  225.5 1.0 collective-permute-start.8
  226.5 0.2 fusion.2
  226.7 4.7 %collective-permute-done.8 = f32[4,32,128]{2,1,0:T(8,128)S(1)} collective-permute-done((f32[4,32,128]{2,1,0:T(8,128)S(1)}, f32[4,32,128]{2,1,0:T(8,128)S(1)}, u32[]{:S(2)}, u32[]{:S(2)}) %collective-permute-start.8) | collective-permute-done | bytes 65568 | tf_op jit(solution)/shard_map/ppermute | solution.py:298
  231.5 1.7 multiply_add_fusion
  (16 shorter events, 0.2 us)
Async XLA Ops:
  1.5 5.2 %copy-start.1 = (f32[64,32,128]{2,1,0:T(8,128)S(1)}, f32[64,32,128]{2,1,0:T(8,128)}, u32[]{:S(2)}) copy-start(f32[64,32,128]{2,1,0:T(8,128)} %own.1) | copy-start | bytes 3145732
  1.5 4.9 %collective-permute-start = (f32[4,32,128]{2,1,0:T(8,128)S(1)}, f32[4,32,128]{2,1,0:T(8,128)S(1)}, u32[]{:S(2)}, u32[]{:S(2)}) collective-permute-start(f32[4,32,128]{2,1,0:T(8,128)S(1)} %slice.59), channel_id=1, source_target_pairs={{0,192},{64,0},{128,64},{192,128},{1,193},{65,1},{129,65},{193,129... | collective-permute-start | bytes 196616 | tf_op jit(solution)/shard_map/ppermute | solution.py:298
  7.1 85.5 %copy-start.4 = (s32[1,3,3]{2,0,1:T(1,128)S(1)}, s32[1,3,3]{2,0,1:T(1,128)}, u32[]{:S(2)}) copy-start(s32[1,3,3]{2,0,1:T(1,128)} %param.11) | copy-start | bytes 112
  92.6 5.8 %copy-start = (f32[64,3,32,128]{3,2,1,0:T(8,128)}, f32[64,3,32,128]{3,2,1,0:T(8,128)S(1)}, u32[]{:S(2)}) copy-start(f32[64,3,32,128]{3,2,1,0:T(8,128)S(1)} %all_to_all.10.boxes) | copy-start | bytes 9437188
  92.6 5.8 %collective-permute-start.1 = (f32[64,3,32,128]{3,2,1,0:T(8,128)S(1)}, f32[64,3,32,128]{3,2,1,0:T(8,128)}, u32[]{:S(2)}, u32[]{:S(2)}) collective-permute-start(f32[64,3,32,128]{3,2,1,0:T(8,128)S(1)} %all_to_all.10.boxes), channel_id=1, source_target_pairs={{0,1},{1,0},{2,3},{3,2},{4,5},{5,4},{6,7},{7,6},{8,9},{9,8},{10,11... | collective-permute-start | bytes 9437192 | tf_op jit(solution)/shard_map/ppermute | solution.py:303
  115.0 6.6 %copy-start.3 = (f32[64,3,32,128]{3,2,1,0:T(8,128)S(1)}, f32[64,3,32,128]{3,2,1,0:T(8,128)}, u32[]{:S(2)}) copy-start(f32[64,3,32,128]{3,2,1,0:T(8,128)} %get-tuple-element.8) | copy-start | bytes 9437188
  115.0 4.6 %collective-permute-start.2 = (f32[64,2,32,128]{3,2,1,0:T(8,128)}, f32[64,2,32,128]{3,2,1,0:T(8,128)}, u32[]{:S(2)}, u32[]{:S(2)}) collective-permute-start(f32[64,2,32,128]{3,2,1,0:T(8,128)} %get-tuple-element.9), channel_id=1, source_target_pairs={{0,1},{1,0},{2,3},{3,2},{4,5},{5,4},{6,7},{7,6},{8,9},{9,8},{10,11... | collective-permute-start | bytes 6291464 | tf_op jit(solution)/shard_map/ppermute | solution.py:303
  115.3 25.7 %collective-permute-start.3 = (f32[64,32,128]{2,1,0:T(8,128)}, f32[64,32,128]{2,1,0:T(8,128)}, u32[]{:S(2)}, u32[]{:S(2)}) collective-permute-start(f32[64,32,128]{2,1,0:T(8,128)} %own.1), channel_id=1, source_target_pairs={{0,2},{1,3},{2,4},{3,5},{4,6},{5,7},{6,8},{7,9},{8,10},{9,11},{10,... | collective-permute-start | bytes 3145736 | tf_op jit(solution)/shard_map/ppermute | solution.py:298
  116.8 25.4 %collective-permute-start.4 = (f32[64,32,128]{2,1,0:T(8,128)}, f32[64,32,128]{2,1,0:T(8,128)}, u32[]{:S(2)}, u32[]{:S(2)}) collective-permute-start(f32[64,32,128]{2,1,0:T(8,128)} %own.1), channel_id=1, source_target_pairs={{0,62},{1,63},{2,0},{3,1},{4,2},{5,3},{6,4},{7,5},{8,6},{9,7},{10,... | collective-permute-start | bytes 3145736 | tf_op jit(solution)/shard_map/ppermute | solution.py:298
  142.2 83.3 %all-to-all-start.1 = ((f32[64,3,32,128]{3,2,1,0:T(8,128)}), f32[64,3,32,128]{3,2,1,0:T(8,128)S(1)}, u32[]{:S(2)}, u32[]{:S(2)}) async-start(f32[64,3,32,128]{3,2,1,0:T(8,128)} %maximum_add_fusion), calls=%async_computation.1 | async-start | bytes 6291456 | tf_op jit(solution)/shard_map/all_to_all | solution.py:334
  151.8 3.1 %collective-permute-start.5 = (f32[64,32,128]{2,1,0:T(8,128)}, f32[64,32,128]{2,1,0:T(8,128)}, u32[]{:S(2)}, u32[]{:S(2)}) collective-permute-start(f32[64,32,128]{2,1,0:T(8,128)} %own.1), channel_id=1, source_target_pairs={{0,1},{1,0},{2,3},{3,2},{4,5},{5,4},{6,7},{7,6},{8,9},{9,8},{10,11... | collective-permute-start | bytes 3145736 | tf_op jit(solution)/shard_map/ppermute | solution.py:303
  152.0 4.4 %collective-permute-start.6 = (f32[64,32,128]{2,1,0:T(8,128)}, f32[64,32,128]{2,1,0:T(8,128)}, u32[]{:S(2)}, u32[]{:S(2)}) collective-permute-start(f32[64,32,128]{2,1,0:T(8,128)} %collective-permute-done.3.low), channel_id=1, source_target_pairs={{0,1},{1,0},{2,3},{3,2},{4,5},{5,4},{6,7},{7,6},{8,9},{9,8},{10,11... | collective-permute-start | bytes 3145736 | tf_op jit(solution)/shard_map/ppermute | solution.py:303
  152.4 5.5 %collective-permute-start.7 = (f32[64,32,128]{2,1,0:T(8,128)}, f32[64,32,128]{2,1,0:T(8,128)}, u32[]{:S(2)}, u32[]{:S(2)}) collective-permute-start(f32[64,32,128]{2,1,0:T(8,128)} %collective-permute-done.4.high), channel_id=1, source_target_pairs={{0,1},{1,0},{2,3},{3,2},{4,5},{5,4},{6,7},{7,6},{8,9},{9,8},{10,11... | collective-permute-start | bytes 3145736 | tf_op jit(solution)/shard_map/ppermute | solution.py:303
  225.5 5.9 %copy-start.2 = (f32[64,32,128]{2,1,0:T(8,128)S(1)}, f32[64,32,128]{2,1,0:T(8,128)}, u32[]{:S(2)}) copy-start(f32[64,32,128]{2,1,0:T(8,128)} %slab.1) | copy-start | bytes 3145732
  225.5 5.9 %collective-permute-start.8 = (f32[4,32,128]{2,1,0:T(8,128)S(1)}, f32[4,32,128]{2,1,0:T(8,128)S(1)}, u32[]{:S(2)}, u32[]{:S(2)}) collective-permute-start(f32[4,32,128]{2,1,0:T(8,128)S(1)} %fusion.3), channel_id=1, source_target_pairs={{0,64},{64,128},{128,192},{192,0},{1,65},{65,129},{129,193},{193,1... | collective-permute-start | bytes 196616 | tf_op jit(solution)/shard_map/ppermute | solution.py:298

commit v4 on v3

--- a/solution.py
+++ b/solution.py
@@ -17,7 +17,7 @@
 PAD = 8
 HIGH = HALF + 2 * PAD
 DEEP = B + 4
-SPAN = 32
+SPAN = 64
 GROUP = 8
 
 coulomb_factor = 4.0 * np.pi
@@ -156,10 +156,10 @@
     return jnp.where(keep, turned, 0.0)
 
 
-def pairs_kernel(place, partners, offsets, mix, boxes, peers, kept, sent,
+def pairs_kernel(scalars, mix, boxes, peers, kept, sent,
                  own, near, rho, work_a, work_b, moved, force, sems, out_sem):
-    core = place[0] & 1
-    dist = [jnp.remainder(partners[0, q] - place[0] + place[1], place[1]) for q in range(3)]
+    core = scalars[0]
+    dist = [scalars[1 + q] for q in range(3)]
     own_copy = pltpu.make_async_copy(boxes.at[:, 0], own, sems.at[3])
     own_copy.start()
     sources = {1: peers.at[:, core], 2: boxes.at[:, 1], 3: peers.at[:, 1 + core], 4: boxes.at[:, 2]}
@@ -171,9 +171,11 @@
     def deliver(which, sem):
         pltpu.make_async_copy(force.at[which], ends[which], sem).start()
 
-    for q in range(3):
+    def fetch_partner(q):
         for far, source in sources.items():
             pl.when(dist[q] == far)(functools.partial(fetch, source, q))
+
+    fetch_partner(0)
     absent = 10 - dist[0] - dist[1] - dist[2]
 
     def blank(a, carry):
@@ -182,8 +184,6 @@
         return carry
 
     lax.fori_loop(0, B, blank, 0, unroll=4)
-    for which in sources:
-        pl.when(absent == which)(functools.partial(deliver, which, out_sem.at[3]))
     for q in range(3):
         clear_edges(near.at[q])
     for buffer in (rho, work_a, work_b):
@@ -197,12 +197,16 @@
     scale = 1.0 / 12.0 / radius
     rows = pl.ds(PAD, HALF)
     own_copy.wait()
+    fetch_partner(1)
+    fetch_partner(2)
+    for which in sources:
+        pl.when(absent == which)(functools.partial(deliver, which, out_sem.at[3]))
 
     def pair(q, carry):
-        offset = (offsets[0, q, 0], offsets[0, q, 1], offsets[0, q, 2])
+        offset = tuple(scalars[4 + 3 * q + k] for k in range(3))
         back = tuple(-o for o in offset)
         partner = near.at[q]
-        target = jnp.where(q == 0, dist[0], jnp.where(q == 1, dist[1], dist[2]))
+        target = scalars[1 + q]
         pltpu.make_async_copy(boxes.at[:, 0], inner_rows(partner), sems.at[q]).wait()
 
         def overlap(a, carry):
@@ -232,17 +236,17 @@
             force[target, a] = shifted_plane(work_a, a, back, upper, cell)
             return carry
 
-        lax.fori_loop(0, B, overlap, 0, unroll=16)
+        lax.fori_loop(0, B, overlap, 0, unroll=64)
         over_spans(sweep_one)
         over_spans(sweep_two)
         over_spans(sweep_three)
-        lax.fori_loop(0, B, give, 0, unroll=16)
+        pl.when(q == 2)(functools.partial(deliver, 0, out_sem.at[4]))
+        lax.fori_loop(0, B, give, 0, unroll=64)
         for which in sources:
             pl.when(target == which)(functools.partial(deliver, which, out_sem.at[q]))
         return carry
 
     lax.fori_loop(0, 3, pair, 0)
-    deliver(0, out_sem.at[4])
     for k in range(5):
         pltpu.make_async_copy(force.at[0], ends[0], out_sem.at[k]).wait()
 
@@ -267,7 +271,7 @@
     )(place, lane_mixers(), *arrays)
 
 
-def pair_forces(place, partners, offsets, boxes, peers):
+def pair_forces(scalars, boxes, peers):
     padded = pltpu.VMEM((DEEP, HIGH, LANES), F32)
     return pl.pallas_call(
         pairs_kernel,
@@ -275,7 +279,7 @@
             jax.ShapeDtypeStruct((B, 3, HALF, LANES), F32),
             jax.ShapeDtypeStruct((B, 2, HALF, LANES), F32),
         ],
-        in_specs=[SCALARS, SCALARS, SCALARS, WHOLE, ANY, ANY],
+        in_specs=[SCALARS, WHOLE, ANY, ANY],
         out_specs=[ANY, ANY],
         scratch_shapes=[
             pltpu.VMEM((B, HALF, LANES), F32),
@@ -290,7 +294,7 @@
         ],
         cost_estimate=pl.CostEstimate(flops=300 * B**3, transcendentals=0, bytes_accessed=40 * B**3),
         name="pairs",
-    )(place, partners, offsets, lane_mixers(), boxes, peers)
+    )(scalars, lane_mixers(), boxes, peers)
 
 
 def from_behind(array, axis, by):
@@ -307,8 +311,10 @@
     slabs = lax.axis_size("grid")
     total = lax.axis_size("orb") * slabs
     index = lax.axis_index("grid")
-    even = (index & 1) == 0
-    place = jnp.stack([lax.axis_index(("orb", "grid")), jnp.int32(total)])
+    core = index & 1
+    place = lax.axis_index(("orb", "grid"))
+    dist = jnp.remainder(partners[0] - place, total)
+    scalars = jnp.concatenate([core[None], dist, offsets.reshape(-1)])
     slab = jnp.stack([index, jnp.int32(slabs)])
 
     upper = from_behind(orbitals[:AHEAD], "orb", -1)
@@ -319,17 +325,10 @@
     source, _ = lax.optimization_barrier((orbitals, boxes))
     low = from_behind(source, "grid", 2)
     high = from_behind(source, "grid", -2)
-    kept, sent = pair_forces(place, partners, offsets, boxes, peers)
+    kept, sent = pair_forces(scalars, boxes, peers)
     given = core_swap(sent)
-    zero = jnp.zeros_like(given[:, 0])
-    summed = kept + jnp.stack(
-        [
-            jnp.where(even, zero, given[:, 0]),
-            jnp.where(even, given[:, 0], given[:, 1]),
-            jnp.where(even, given[:, 1], zero),
-        ],
-        axis=1,
-    )
+    padded = jnp.pad(given, ((0, 0), (1, 1), (0, 0), (0, 0)))
+    summed = kept + lax.dynamic_slice_in_dim(padded, core, 3, axis=1)
     summed, low, high = lax.optimization_barrier((summed, low, high))
     returned = lax.all_to_all(summed, "grid", split_axis=0, concat_axis=0, tiled=True)
     sides = [core_swap(array) for array in (source, low, high)]

time: 234 us -> 231 us (0.987)
  Pallas kernels: 24.3 us -> 21.5 us
    pallas_call x1, Pallas kernels: 16.6 us -> 13.8 us  [pair_forces(): pl.pallas_call(pairs_kernel, out_shape=[jax.ShapeDtypeStruct((B, 3, HALF,...]
where the time goes in v4:
time: 231 us; the launch traced here: 230 us
  waiting for transfers between devices  95.5 us (41%)
  blocking collectives  85.5 us (37%)
  Pallas kernels  21.5 us (9%)
  starting transfers between devices  16.5 us (7%)
  other arithmetic  8 us (3%)
  local copies, waits for them, and re-layouts  2.51 us (1%)
    all_to_all x1, blocking collectives, local(): lax.all_to_all(windows, 'grid', split_axis=0, concat_axis=0, tiled=True)  85.5 us
    all_to_all x1, waiting for transfers between devices, local(): lax.all_to_all(summed, 'grid', split_axis=0, concat_axis=0, tiled=True)  59.9 us
    ppermute x4, waiting for transfers between devices, from_behind(): lax.ppermute(array, axis, [(i, (i + by) % count) for i in range(count)])  23.7 us
    pallas_call x1, Pallas kernels, pair_forces(): pl.pallas_call(pairs_kernel, out_shape=[jax.ShapeDtypeStruct((B, 3, HALF,...  13.8 us
    ppermute x5, waiting for transfers between devices, core_swap(): return lax.ppermute(array, 'grid', [(i, i ^ 1) for i in range(count)])  11.9 us
    all_to_all x1, starting transfers between devices, local(): lax.all_to_all(summed, 'grid', split_axis=0, concat_axis=0, tiled=True)  9.57 us
    pallas_call x1, Pallas kernels, slab_terms(): pl.pallas_call(slab_kernel, grid=(arrays[0].shape[0] // GROUP,), out_shap...  7.73 us
    ppermute x4, starting transfers between devices, from_behind(): lax.ppermute(array, axis, [(i, (i + by) % count) for i in range(count)])  6.03 us
  transfers between devices with their start and end apart: 10, of which 10 were waited for; matrix products, arithmetic and copies ran while one was open for 3% of the time, Pallas kernels for 3%

profile of v4, /device:TPU:2, one launch (start us, length us, event | category | flops | bytes accessed | tf_op | source)
XLA Modules:
  0.0 230.3 jit_solution(12435708494951232730)
XLA Ops:
  0.6 0.8 slice.51
  1.5 3.0 %collective-permute-start = (f32[4,32,128]{2,1,0:T(8,128)S(1)}, f32[4,32,128]{2,1,0:T(8,128)S(1)}, u32[]{:S(2)}, u32[]{:S(2)}) collective-permute-start(f32[4,32,128]{2,1,0:T(8,128)S(1)} %slice.51), channel_id=1, source_target_pairs={{0,192},{64,0},{128,64},{192,128},{1,193},{65,1},{129,65},{193,129... | collective-permute-start | bytes 196616 | tf_op jit(solution)/shard_map/ppermute | solution.py:302
  4.5 1.3 constant_dynamic-update-slice_fusion.1
  5.8 0.6 collective-permute-done
  6.4 0.2 slice_bitcast_fusion.2
  6.7 0.4 pad_maximum_fusion
  7.1 85.5 %all_to_all.10.boxes = f32[64,3,32,128]{3,2,1,0:T(8,128)S(1)} all-to-all(f32[64,3,32,128]{3,2,1,0:T(8,128)S(1)} %pad_maximum_fusion), channel_id=1, replica_groups=mesh['orb'=4,'grid'=64] {'grid'}, dimensions={0} | all-to-all | bytes 6291456 | tf_op jit(solution)/shard_map/all_to_all | solution.py:323
  92.7 0.1 reshape.15
  92.8 0.8 pad_add_fusion.1.scalars
  93.5 4.9 %collective-permute-done.1.peers = f32[64,3,32,128]{3,2,1,0:T(8,128)} collective-permute-done((f32[64,3,32,128]{3,2,1,0:T(8,128)S(1)}, f32[64,3,32,128]{3,2,1,0:T(8,128)}, u32[]{:S(2)}, u32[]{:S(2)}) %collective-permute-start.1) | collective-permute-done | bytes 3145760 | tf_op jit(solution)/shard_map/ppermute | solution.py:307
  98.4 13.8 %pairs.1 = (f32[64,3,32,128]{3,2,1,0:T(8,128)}, f32[64,2,32,128]{3,2,1,0:T(8,128)}) custom-call(s32[13]{0:T(128)} %pad_add_fusion.1.scalars, bf16[512,128]{1,0:T(8,128)(2,1)} %constant.39.clone.mix, f32[64,3,32,128]{3,2,1,0:T(8,128)} %copy-done, f32[64,3,32,128]{3,2,1,0:T(8,128)} %collective-permute-done.1.peers), custom_call_target="tpu_custom_call" | custom-call | flops 78643200 | bytes 10485760 | tf_op jit(solution)/shard_map/pairs/pallas_call | solution.py:276
  112.2 0.2 collective-permute-start.2
  112.4 1.6 collective-permute-start.3
  114.0 0.5 collective-permute-start.4
  114.5 2.2 collective-permute-done.2
  116.7 4.3 %fusion = f32[64,3,32,128]{3,2,1,0:T(8,128)} fusion(f32[64,3,32,128]{3,2,1,0:T(8,128)} %get-tuple-element.8, s32[]{:T(128)S(6)} %select_n.11, f32[64,2,32,128]{3,2,1,0:T(8,128)S(1)} %collective-permute-done.2), kind=kLoop, calls=%fused_computation.1 | loop fusion | flops 786432 | bytes 8388612 | tf_op jit(solution)/shard_map/add | solution.py:331
  121.0 17.1 %collective-permute-done.3.low = f32[64,32,128]{2,1,0:T(8,128)S(1)} collective-permute-done((f32[64,32,128]{2,1,0:T(8,128)}, f32[64,32,128]{2,1,0:T(8,128)S(1)}, u32[]{:S(2)}, u32[]{:S(2)}) %collective-permute-start.3) | collective-permute-done | bytes 1048608 | tf_op jit(solution)/shard_map/ppermute | solution.py:302
  138.1 1.3 collective-permute-done.4.high
  139.4 9.6 %all-to-all-start.1 = ((f32[64,3,32,128]{3,2,1,0:T(8,128)}), f32[64,3,32,128]{3,2,1,0:T(8,128)S(1)}, u32[]{:S(2)}, u32[]{:S(2)}) async-start(f32[64,3,32,128]{3,2,1,0:T(8,128)} %fusion), calls=%async_computation.1 | async-start | bytes 6291456 | tf_op jit(solution)/shard_map/all_to_all | solution.py:333
  149.0 0.2 collective-permute-start.5
  149.2 0.4 collective-permute-start.6
  149.6 0.1 collective-permute-start.7
  149.7 0.6 pad_add_fusion.place
  150.3 1.8 collective-permute-done.5.peer
  152.1 1.5 collective-permute-done.6.peer_low
  153.6 1.5 collective-permute-done.7.peer_high
  155.1 7.7 %slab.1 = f32[64,32,128]{2,1,0:T(8,128)} custom-call(s32[2]{0:T(128)} %pad_add_fusion.place, bf16[512,128]{1,0:T(8,128)(2,1)} %constant.39.clone.mix, f32[64,32,128]{2,1,0:T(8,128)} %own.1, f32[64,32,128]{2,1,0:T(8,128)} %copy-done.3, f32[64,32,128]{2,1,0:T(8,128)} %collective-permute-done.4.high, f32[64,32,128]{2,1,0:T(8,128)} %collective-permute-done.5.peer, ...), custom_call_target="tpu_custom_call" | custom-call | flops 5242880 | bytes 9437184 | tf_op jit(solution)/shard_map/slab/pallas_call | solution.py:262
  162.8 59.9 %all-to-all-done.1 = f32[64,3,32,128]{3,2,1,0:T(8,128)S(1)} async-done(((f32[64,3,32,128]{3,2,1,0:T(8,128)}), f32[64,3,32,128]{3,2,1,0:T(8,128)S(1)}, u32[]{:S(2)}, u32[]{:S(2)}) %all-to-all-start.1) | async-done | bytes 3145760 | tf_op jit(solution)/shard_map/all_to_all | solution.py:333
  222.7 1.0 collective-permute-start.8
  223.7 0.2 fusion.3
  223.9 4.7 %collective-permute-done.8 = f32[4,32,128]{2,1,0:T(8,128)S(1)} collective-permute-done((f32[4,32,128]{2,1,0:T(8,128)S(1)}, f32[4,32,128]{2,1,0:T(8,128)S(1)}, u32[]{:S(2)}, u32[]{:S(2)}) %collective-permute-start.8) | collective-permute-done | bytes 65568 | tf_op jit(solution)/shard_map/ppermute | solution.py:302
  228.6 1.7 multiply_add_fusion
  (19 shorter events, 0.1 us)
Async XLA Ops:
  1.5 5.2 %copy-start.1 = (f32[64,32,128]{2,1,0:T(8,128)S(1)}, f32[64,32,128]{2,1,0:T(8,128)}, u32[]{:S(2)}) copy-start(f32[64,32,128]{2,1,0:T(8,128)} %own.1) | copy-start | bytes 3145732
  1.5 4.9 %collective-permute-start = (f32[4,32,128]{2,1,0:T(8,128)S(1)}, f32[4,32,128]{2,1,0:T(8,128)S(1)}, u32[]{:S(2)}, u32[]{:S(2)}) collective-permute-start(f32[4,32,128]{2,1,0:T(8,128)S(1)} %slice.51), channel_id=1, source_target_pairs={{0,192},{64,0},{128,64},{192,128},{1,193},{65,1},{129,65},{193,129... | collective-permute-start | bytes 196616 | tf_op jit(solution)/shard_map/ppermute | solution.py:302
  7.1 85.6 %copy-start.4 = (s32[1,3,3]{2,0,1:T(1,128)S(1)}, s32[1,3,3]{2,0,1:T(1,128)}, u32[]{:S(2)}) copy-start(s32[1,3,3]{2,0,1:T(1,128)} %param.11) | copy-start | bytes 112
  7.1 85.7 %copy-start.5 = (s32[1,3]{1,0:T(1,128)S(1)}, s32[1,3]{1,0:T(1,128)}, u32[]{:S(2)}) copy-start(s32[1,3]{1,0:T(1,128)} %param.10) | copy-start | bytes 40
  92.6 5.8 %copy-start = (f32[64,3,32,128]{3,2,1,0:T(8,128)}, f32[64,3,32,128]{3,2,1,0:T(8,128)S(1)}, u32[]{:S(2)}) copy-start(f32[64,3,32,128]{3,2,1,0:T(8,128)S(1)} %all_to_all.10.boxes) | copy-start | bytes 9437188
  92.6 5.8 %collective-permute-start.1 = (f32[64,3,32,128]{3,2,1,0:T(8,128)S(1)}, f32[64,3,32,128]{3,2,1,0:T(8,128)}, u32[]{:S(2)}, u32[]{:S(2)}) collective-permute-start(f32[64,3,32,128]{3,2,1,0:T(8,128)S(1)} %all_to_all.10.boxes), channel_id=1, source_target_pairs={{0,1},{1,0},{2,3},{3,2},{4,5},{5,4},{6,7},{7,6},{8,9},{9,8},{10,11... | collective-permute-start | bytes 9437192 | tf_op jit(solution)/shard_map/ppermute | solution.py:307
  112.2 4.5 %collective-permute-start.2 = (f32[64,2,32,128]{3,2,1,0:T(8,128)}, f32[64,2,32,128]{3,2,1,0:T(8,128)S(1)}, u32[]{:S(2)}, u32[]{:S(2)}) collective-permute-start(f32[64,2,32,128]{3,2,1,0:T(8,128)} %get-tuple-element.9), channel_id=1, source_target_pairs={{0,1},{1,0},{2,3},{3,2},{4,5},{5,4},{6,7},{7,6},{8,9},{9,8},{10,11... | collective-permute-start | bytes 6291464 | tf_op jit(solution)/shard_map/ppermute | solution.py:307
  112.4 25.7 %collective-permute-start.3 = (f32[64,32,128]{2,1,0:T(8,128)}, f32[64,32,128]{2,1,0:T(8,128)S(1)}, u32[]{:S(2)}, u32[]{:S(2)}) collective-permute-start(f32[64,32,128]{2,1,0:T(8,128)} %own.1), channel_id=1, source_target_pairs={{0,2},{1,3},{2,4},{3,5},{4,6},{5,7},{6,8},{7,9},{8,10},{9,11},{10,... | collective-permute-start | bytes 3145736 | tf_op jit(solution)/shard_map/ppermute | solution.py:302
  114.0 25.4 %collective-permute-start.4 = (f32[64,32,128]{2,1,0:T(8,128)}, f32[64,32,128]{2,1,0:T(8,128)}, u32[]{:S(2)}, u32[]{:S(2)}) collective-permute-start(f32[64,32,128]{2,1,0:T(8,128)} %own.1), channel_id=1, source_target_pairs={{0,62},{1,63},{2,0},{3,1},{4,2},{5,3},{6,4},{7,5},{8,6},{9,7},{10,... | collective-permute-start | bytes 3145736 | tf_op jit(solution)/shard_map/ppermute | solution.py:302
  138.1 1.3 copy-start.3
  139.4 83.3 %all-to-all-start.1 = ((f32[64,3,32,128]{3,2,1,0:T(8,128)}), f32[64,3,32,128]{3,2,1,0:T(8,128)S(1)}, u32[]{:S(2)}, u32[]{:S(2)}) async-start(f32[64,3,32,128]{3,2,1,0:T(8,128)} %fusion), calls=%async_computation.1 | async-start | bytes 6291456 | tf_op jit(solution)/shard_map/all_to_all | solution.py:333
  149.0 3.1 %collective-permute-start.5 = (f32[64,32,128]{2,1,0:T(8,128)}, f32[64,32,128]{2,1,0:T(8,128)}, u32[]{:S(2)}, u32[]{:S(2)}) collective-permute-start(f32[64,32,128]{2,1,0:T(8,128)} %own.1), channel_id=1, source_target_pairs={{0,1},{1,0},{2,3},{3,2},{4,5},{5,4},{6,7},{7,6},{8,9},{9,8},{10,11... | collective-permute-start | bytes 3145736 | tf_op jit(solution)/shard_map/ppermute | solution.py:307
  149.2 4.4 %collective-permute-start.6 = (f32[64,32,128]{2,1,0:T(8,128)}, f32[64,32,128]{2,1,0:T(8,128)}, u32[]{:S(2)}, u32[]{:S(2)}) collective-permute-start(f32[64,32,128]{2,1,0:T(8,128)} %copy-done.3), channel_id=1, source_target_pairs={{0,1},{1,0},{2,3},{3,2},{4,5},{5,4},{6,7},{7,6},{8,9},{9,8},{10,11... | collective-permute-start | bytes 3145736 | tf_op jit(solution)/shard_map/ppermute | solution.py:307
  149.6 5.5 %collective-permute-start.7 = (f32[64,32,128]{2,1,0:T(8,128)}, f32[64,32,128]{2,1,0:T(8,128)}, u32[]{:S(2)}, u32[]{:S(2)}) collective-permute-start(f32[64,32,128]{2,1,0:T(8,128)} %collective-permute-done.4.high), channel_id=1, source_target_pairs={{0,1},{1,0},{2,3},{3,2},{4,5},{5,4},{6,7},{7,6},{8,9},{9,8},{10,11... | collective-permute-start | bytes 3145736 | tf_op jit(solution)/shard_map/ppermute | solution.py:307
  222.7 5.9 %copy-start.2 = (f32[64,32,128]{2,1,0:T(8,128)S(1)}, f32[64,32,128]{2,1,0:T(8,128)}, u32[]{:S(2)}) copy-start(f32[64,32,128]{2,1,0:T(8,128)} %slab.1) | copy-start | bytes 3145732
  222.7 5.9 %collective-permute-start.8 = (f32[4,32,128]{2,1,0:T(8,128)S(1)}, f32[4,32,128]{2,1,0:T(8,128)S(1)}, u32[]{:S(2)}, u32[]{:S(2)}) collective-permute-start(f32[4,32,128]{2,1,0:T(8,128)S(1)} %fusion.4), channel_id=1, source_target_pairs={{0,64},{64,128},{128,192},{192,0},{1,65},{65,129},{129,193},{193,1... | collective-permute-start | bytes 196616 | tf_op jit(solution)/shard_map/ppermute | solution.py:302

commit v5 on v4

--- a/solution.py
+++ b/solution.py
@@ -320,6 +320,7 @@
     upper = from_behind(orbitals[:AHEAD], "orb", -1)
     longer = jnp.concatenate([orbitals, upper], axis=0)
     windows = jnp.stack([longer[:slabs], longer[2 : 2 + slabs], longer[4 : 4 + slabs]], axis=1)
+    windows, scalars = lax.optimization_barrier((windows, scalars))
     boxes = lax.all_to_all(windows, "grid", split_axis=0, concat_axis=0, tiled=True)
     peers = core_swap(boxes)
     source, _ = lax.optimization_barrier((orbitals, boxes))
@@ -327,9 +328,9 @@
     high = from_behind(source, "grid", -2)
     kept, sent = pair_forces(scalars, boxes, peers)
     given = core_swap(sent)
-    padded = jnp.pad(given, ((0, 0), (1, 1), (0, 0), (0, 0)))
-    summed = kept + lax.dynamic_slice_in_dim(padded, core, 3, axis=1)
-    summed, low, high = lax.optimization_barrier((summed, low, high))
+    summed = lax.dynamic_update_slice_in_dim(
+        kept, lax.dynamic_slice_in_dim(kept, 1 - core, 2, axis=1) + given, 1 - core, axis=1
+    )
     returned = lax.all_to_all(summed, "grid", split_axis=0, concat_axis=0, tiled=True)
     sides = [core_swap(array) for array in (source, low, high)]
     base = slab_terms(slab, [orbitals, low, high, *sides, previous, potential])

time: 231 us -> 244 us (1.056)
  the two profiles are of different devices: /device:TPU:2 before, /device:TPU:1 now
where the time goes in v5:
time: 244 us; the launch traced here: 243 us
  waiting for transfers between devices  105 us (43%)
  blocking collectives  85.4 us (35%)
  Pallas kernels  21.5 us (9%)
  starting transfers between devices  17.5 us (7%)
  other arithmetic  8.39 us (3%)
  local copies, waits for them, and re-layouts  4.55 us (2%)
    ppermute x4, waiting for transfers between devices, from_behind(): lax.ppermute(array, axis, [(i, (i + by) % count) for i in range(count)])  93.6 us
    all_to_all x1, blocking collectives, local(): lax.all_to_all(windows, 'grid', split_axis=0, concat_axis=0, tiled=True)  85.4 us
    pallas_call x1, Pallas kernels, pair_forces(): pl.pallas_call(pairs_kernel, out_shape=[jax.ShapeDtypeStruct((B, 3, HALF,...  13.7 us
    ppermute x5, waiting for transfers between devices, core_swap(): return lax.ppermute(array, 'grid', [(i, i ^ 1) for i in range(count)])  11.5 us
    ppermute x4, starting transfers between devices, from_behind(): lax.ppermute(array, axis, [(i, (i + by) % count) for i in range(count)])  8.79 us
    pallas_call x1, Pallas kernels, slab_terms(): pl.pallas_call(slab_kernel, grid=(arrays[0].shape[0] // GROUP,), out_shap...  7.72 us
    all_to_all x1, starting transfers between devices, local(): lax.all_to_all(summed, 'grid', split_axis=0, concat_axis=0, tiled=True)  5.35 us
  transfers between devices with their start and end apart: 10, of which 6 were waited for; matrix products, arithmetic and copies ran while one was open for 2% of the time, Pallas kernels for 3%

profile of v5, /device:TPU:1, one launch (start us, length us, event | category | flops | bytes accessed | tf_op | source)
XLA Modules:
  0.0 243.2 jit_solution(17401822940224875918)
XLA Ops:
  0.6 0.8 slice.51
  1.5 3.6 %collective-permute-start = (f32[4,32,128]{2,1,0:T(8,128)S(1)}, f32[4,32,128]{2,1,0:T(8,128)S(1)}, u32[]{:S(2)}, u32[]{:S(2)}) collective-permute-start(f32[4,32,128]{2,1,0:T(8,128)S(1)} %slice.51), channel_id=1, source_target_pairs={{0,192},{64,0},{128,64},{192,128},{1,193},{65,1},{129,65},{193,129... | collective-permute-start | bytes 196616 | tf_op jit(solution)/shard_map/ppermute | solution.py:302
  5.0 1.4 constant_dynamic-update-slice_fusion.1
  6.4 0.7 reduce
  7.1 0.1 reshape.15
  7.2 0.7 and_select_fusion
  7.9 0.6 pad_add_fusion.1.scalars
  8.5 0.3 slice_bitcast_fusion.2
  8.7 0.4 pad_maximum_fusion
  9.1 85.4 %all_to_all.10.boxes = f32[64,3,32,128]{3,2,1,0:T(8,128)S(1)} all-to-all(f32[64,3,32,128]{3,2,1,0:T(8,128)S(1)} %pad_maximum_fusion), channel_id=1, replica_groups=mesh['orb'=4,'grid'=64] {'grid'}, dimensions={0} | all-to-all | bytes 6291456 | tf_op jit(solution)/shard_map/all_to_all | solution.py:324
  94.5 1.1 collective-permute-start.6
  95.6 5.4 %collective-permute-done.6.peers = f32[64,3,32,128]{3,2,1,0:T(8,128)} collective-permute-done((f32[64,3,32,128]{3,2,1,0:T(8,128)S(1)}, f32[64,3,32,128]{3,2,1,0:T(8,128)}, u32[]{:S(2)}, u32[]{:S(2)}) %collective-permute-start.6) | collective-permute-done | bytes 3145760 | tf_op jit(solution)/shard_map/ppermute | solution.py:307
  101.1 13.7 %pairs.1 = (f32[64,3,32,128]{3,2,1,0:T(8,128)}, f32[64,2,32,128]{3,2,1,0:T(8,128)}) custom-call(s32[13]{0:T(128)} %pad_add_fusion.1.scalars, bf16[512,128]{1,0:T(8,128)(2,1)} %constant.40.clone.mix, f32[64,3,32,128]{3,2,1,0:T(8,128)} %copy-done, f32[64,3,32,128]{3,2,1,0:T(8,128)} %collective-permute-done.6.peers), custom_call_target="tpu_custom_call" | custom-call | flops 78643200 | bytes 10485760 | tf_op jit(solution)/shard_map/pairs/pallas_call | solution.py:276
  114.8 0.5 collective-permute-start.7
  115.3 4.0 %collective-permute-done.7 = f32[64,2,32,128]{3,2,1,0:T(8,128)S(1)} collective-permute-done((f32[64,2,32,128]{3,2,1,0:T(8,128)}, f32[64,2,32,128]{3,2,1,0:T(8,128)S(1)}, u32[]{:S(2)}, u32[]{:S(2)}) %collective-permute-start.7) | collective-permute-done | bytes 2097184 | tf_op jit(solution)/shard_map/ppermute | solution.py:307
  119.3 3.4 %add_dynamic-update-slice_fusion = f32[64,3,32,128]{3,2,1,0:T(8,128)} fusion(f32[64,3,32,128]{3,2,1,0:T(8,128)} %get-tuple-element.10, s32[]{:T(128)S(6)} %select_n.12, f32[64,2,32,128]{3,2,1,0:T(8,128)S(1)} %collective-permute-done.7), kind=kLoop, calls=%fused_computation.1 | loop fusion | flops 524288 | bytes 6291460 | tf_op jit(solution)/shard_map/dynamic_update_slice | solution.py:331
  122.8 5.4 %all-to-all-start.1 = ((f32[64,3,32,128]{3,2,1,0:T(8,128)}), f32[64,3,32,128]{3,2,1,0:T(8,128)S(1)}, u32[]{:S(2)}, u32[]{:S(2)}) async-start(f32[64,3,32,128]{3,2,1,0:T(8,128)} %add_dynamic-update-slice_fusion), calls=%async_computation.1 | async-start | bytes 6291456 | tf_op jit(solution)/shard_map/all_to_all | solution.py:334
  128.1 1.4 collective-permute-start.1
  129.5 3.7 %collective-permute-start.2 = (f32[64,32,128]{2,1,0:T(8,128)}, f32[64,32,128]{2,1,0:T(8,128)S(1)}, u32[]{:S(2)}, u32[]{:S(2)}) collective-permute-start(f32[64,32,128]{2,1,0:T(8,128)} %own.1), channel_id=1, source_target_pairs={{0,62},{1,63},{2,0},{3,1},{4,2},{5,3},{6,4},{7,5},{8,6},{9,7},{10,... | collective-permute-start | bytes 3145736 | tf_op jit(solution)/shard_map/ppermute | solution.py:302
  133.3 0.7 collective-permute-start.3
  134.0 89.5 %collective-permute-done.1.low = f32[64,32,128]{2,1,0:T(8,128)S(1)} collective-permute-done((f32[64,32,128]{2,1,0:T(8,128)}, f32[64,32,128]{2,1,0:T(8,128)S(1)}, u32[]{:S(2)}, u32[]{:S(2)}) %collective-permute-start.1) | collective-permute-done | bytes 1048608 | tf_op jit(solution)/shard_map/ppermute | solution.py:302
  223.5 1.0 copy-done.3
  224.5 1.0 collective-permute-start.4
  225.4 0.1 collective-permute-start.5
  225.5 0.7 pad_add_fusion.place
  226.2 1.5 collective-permute-done.4.peer_low
  227.7 1.0 copy-done.6
  228.7 0.6 collective-permute-done.5.peer_high
  229.3 7.7 %slab.1 = f32[64,32,128]{2,1,0:T(8,128)} custom-call(s32[2]{0:T(128)} %pad_add_fusion.place, bf16[512,128]{1,0:T(8,128)(2,1)} %constant.40.clone.mix, f32[64,32,128]{2,1,0:T(8,128)} %own.1, f32[64,32,128]{2,1,0:T(8,128)} %copy-done.3, f32[64,32,128]{2,1,0:T(8,128)} %copy-done.4, f32[64,32,128]{2,1,0:T(8,128)} %copy-done.5, f32[64,32,128]{2,1,0:T(8,128)} %copy-done.6, ...), custom_call_target="tpu_custom_call" | custom-call | flops 5242880 | bytes 9437184 | tf_op jit(solution)/shard_map/slab/pallas_call | solution.py:262
  237.2 0.2 fusion.1
  237.4 4.1 %collective-permute-done.8 = f32[4,32,128]{2,1,0:T(8,128)S(1)} collective-permute-done((f32[4,32,128]{2,1,0:T(8,128)S(1)}, f32[4,32,128]{2,1,0:T(8,128)S(1)}, u32[]{:S(2)}, u32[]{:S(2)}) %collective-permute-start.8) | collective-permute-done | bytes 65568 | tf_op jit(solution)/shard_map/ppermute | solution.py:302
  241.5 1.7 multiply_add_fusion
  (21 shorter events, 0.1 us)
Async XLA Ops:
  1.5 7.0 %collective-permute-start = (f32[4,32,128]{2,1,0:T(8,128)S(1)}, f32[4,32,128]{2,1,0:T(8,128)S(1)}, u32[]{:S(2)}, u32[]{:S(2)}) collective-permute-start(f32[4,32,128]{2,1,0:T(8,128)S(1)} %slice.51), channel_id=1, source_target_pairs={{0,192},{64,0},{128,64},{192,128},{1,193},{65,1},{129,65},{193,129... | collective-permute-start | bytes 196616 | tf_op jit(solution)/shard_map/ppermute | solution.py:302
  5.0 3.7 %copy-start.1 = (f32[64,32,128]{2,1,0:T(8,128)S(1)}, f32[64,32,128]{2,1,0:T(8,128)}, u32[]{:S(2)}) copy-start(f32[64,32,128]{2,1,0:T(8,128)} %own.1) | copy-start | bytes 3145732
  94.5 6.5 %copy-start = (f32[64,3,32,128]{3,2,1,0:T(8,128)}, f32[64,3,32,128]{3,2,1,0:T(8,128)S(1)}, u32[]{:S(2)}) copy-start(f32[64,3,32,128]{3,2,1,0:T(8,128)S(1)} %all_to_all.10.boxes) | copy-start | bytes 9437188
  94.5 6.5 %collective-permute-start.6 = (f32[64,3,32,128]{3,2,1,0:T(8,128)S(1)}, f32[64,3,32,128]{3,2,1,0:T(8,128)}, u32[]{:S(2)}, u32[]{:S(2)}) collective-permute-start(f32[64,3,32,128]{3,2,1,0:T(8,128)S(1)} %all_to_all.10.boxes), channel_id=1, source_target_pairs={{0,1},{1,0},{2,3},{3,2},{4,5},{5,4},{6,7},{7,6},{8,9},{9,8},{10,11... | collective-permute-start | bytes 9437192 | tf_op jit(solution)/shard_map/ppermute | solution.py:307
  114.8 4.5 %collective-permute-start.7 = (f32[64,2,32,128]{3,2,1,0:T(8,128)}, f32[64,2,32,128]{3,2,1,0:T(8,128)S(1)}, u32[]{:S(2)}, u32[]{:S(2)}) collective-permute-start(f32[64,2,32,128]{3,2,1,0:T(8,128)} %get-tuple-element.11), channel_id=1, source_target_pairs={{0,1},{1,0},{2,3},{3,2},{4,5},{5,4},{6,7},{7,6},{8,9},{9,8},{10,11... | collective-permute-start | bytes 6291464 | tf_op jit(solution)/shard_map/ppermute | solution.py:307
  122.8 114.3 %all-to-all-start.1 = ((f32[64,3,32,128]{3,2,1,0:T(8,128)}), f32[64,3,32,128]{3,2,1,0:T(8,128)S(1)}, u32[]{:S(2)}, u32[]{:S(2)}) async-start(f32[64,3,32,128]{3,2,1,0:T(8,128)} %add_dynamic-update-slice_fusion), calls=%async_computation.1 | async-start | bytes 6291456 | tf_op jit(solution)/shard_map/all_to_all | solution.py:334
  128.1 95.4 %collective-permute-start.1 = (f32[64,32,128]{2,1,0:T(8,128)}, f32[64,32,128]{2,1,0:T(8,128)S(1)}, u32[]{:S(2)}, u32[]{:S(2)}) collective-permute-start(f32[64,32,128]{2,1,0:T(8,128)} %own.1), channel_id=1, source_target_pairs={{0,2},{1,3},{2,4},{3,5},{4,6},{5,7},{6,8},{7,9},{8,10},{9,11},{10,... | collective-permute-start | bytes 3145736 | tf_op jit(solution)/shard_map/ppermute | solution.py:302
  129.5 95.9 %collective-permute-start.2 = (f32[64,32,128]{2,1,0:T(8,128)}, f32[64,32,128]{2,1,0:T(8,128)S(1)}, u32[]{:S(2)}, u32[]{:S(2)}) collective-permute-start(f32[64,32,128]{2,1,0:T(8,128)} %own.1), channel_id=1, source_target_pairs={{0,62},{1,63},{2,0},{3,1},{4,2},{5,3},{6,4},{7,5},{8,6},{9,7},{10,... | collective-permute-start | bytes 3145736 | tf_op jit(solution)/shard_map/ppermute | solution.py:302
  133.3 93.0 %collective-permute-start.3 = (f32[64,32,128]{2,1,0:T(8,128)}, f32[64,32,128]{2,1,0:T(8,128)S(1)}, u32[]{:S(2)}, u32[]{:S(2)}) collective-permute-start(f32[64,32,128]{2,1,0:T(8,128)} %own.1), channel_id=1, source_target_pairs={{0,1},{1,0},{2,3},{3,2},{4,5},{5,4},{6,7},{7,6},{8,9},{9,8},{10,11... | collective-permute-start | bytes 3145736 | tf_op jit(solution)/shard_map/ppermute | solution.py:307
  223.5 1.0 copy-start.3
  224.5 3.3 %collective-permute-start.4 = (f32[64,32,128]{2,1,0:T(8,128)S(1)}, f32[64,32,128]{2,1,0:T(8,128)S(1)}, u32[]{:S(2)}, u32[]{:S(2)}) collective-permute-start(f32[64,32,128]{2,1,0:T(8,128)S(1)} %collective-permute-done.1.low), channel_id=1, source_target_pairs={{0,1},{1,0},{2,3},{3,2},{4,5},{5,4},{6,7},{7,6},{8,9},{9,8},{10,11... | collective-permute-start | bytes 3145736 | tf_op jit(solution)/shard_map/ppermute | solution.py:307
  225.4 2.3 copy-start.4
  225.4 3.9 %collective-permute-start.5 = (f32[64,32,128]{2,1,0:T(8,128)S(1)}, f32[64,32,128]{2,1,0:T(8,128)}, u32[]{:S(2)}, u32[]{:S(2)}) collective-permute-start(f32[64,32,128]{2,1,0:T(8,128)S(1)} %collective-permute-done.2.high), channel_id=1, source_target_pairs={{0,1},{1,0},{2,3},{3,2},{4,5},{5,4},{6,7},{7,6},{8,9},{9,8},{10,11... | collective-permute-start | bytes 3145736 | tf_op jit(solution)/shard_map/ppermute | solution.py:307
  226.2 1.5 copy-start.5
  227.7 1.0 copy-start.6
  237.1 4.5 %copy-start.2 = (f32[64,32,128]{2,1,0:T(8,128)S(1)}, f32[64,32,128]{2,1,0:T(8,128)}, u32[]{:S(2)}) copy-start(f32[64,32,128]{2,1,0:T(8,128)} %slab.1) | copy-start | bytes 3145732
  237.1 4.4 %collective-permute-start.8 = (f32[4,32,128]{2,1,0:T(8,128)S(1)}, f32[4,32,128]{2,1,0:T(8,128)S(1)}, u32[]{:S(2)}, u32[]{:S(2)}) collective-permute-start(f32[4,32,128]{2,1,0:T(8,128)S(1)} %fusion.2), channel_id=1, source_target_pairs={{0,64},{64,128},{128,192},{192,0},{1,65},{65,129},{129,193},{193,1... | collective-permute-start | bytes 196616 | tf_op jit(solution)/shard_map/ppermute | solution.py:302

commit v6 on v5

--- a/solution.py
+++ b/solution.py
@@ -156,10 +156,12 @@
     return jnp.where(keep, turned, 0.0)
 
 
-def pairs_kernel(scalars, mix, boxes, peers, kept, sent,
+def pairs_kernel(partners, offsets, mix, boxes, peers, kept, sent,
                  own, near, rho, work_a, work_b, moved, force, sems, out_sem):
-    core = scalars[0]
-    dist = [scalars[1 + q] for q in range(3)]
+    core = lax.axis_index("grid") & 1
+    total = lax.axis_size("orb") * lax.axis_size("grid")
+    place = lax.axis_index("orb") * lax.axis_size("grid") + lax.axis_index("grid")
+    dist = [lax.rem(partners[0, q] - place + total, total) for q in range(3)]
     own_copy = pltpu.make_async_copy(boxes.at[:, 0], own, sems.at[3])
     own_copy.start()
     sources = {1: peers.at[:, core], 2: boxes.at[:, 1], 3: peers.at[:, 1 + core], 4: boxes.at[:, 2]}
@@ -203,10 +205,10 @@
         pl.when(absent == which)(functools.partial(deliver, which, out_sem.at[3]))
 
     def pair(q, carry):
-        offset = tuple(scalars[4 + 3 * q + k] for k in range(3))
+        offset = tuple(offsets[0, q, k] for k in range(3))
         back = tuple(-o for o in offset)
         partner = near.at[q]
-        target = scalars[1 + q]
+        target = jnp.where(q == 0, dist[0], jnp.where(q == 1, dist[1], dist[2]))
         pltpu.make_async_copy(boxes.at[:, 0], inner_rows(partner), sems.at[q]).wait()
 
         def overlap(a, carry):
@@ -271,7 +273,7 @@
     )(place, lane_mixers(), *arrays)
 
 
-def pair_forces(scalars, boxes, peers):
+def pair_forces(partners, offsets, boxes, peers):
     padded = pltpu.VMEM((DEEP, HIGH, LANES), F32)
     return pl.pallas_call(
         pairs_kernel,
@@ -279,7 +281,7 @@
             jax.ShapeDtypeStruct((B, 3, HALF, LANES), F32),
             jax.ShapeDtypeStruct((B, 2, HALF, LANES), F32),
         ],
-        in_specs=[SCALARS, WHOLE, ANY, ANY],
+        in_specs=[SCALARS, SCALARS, WHOLE, ANY, ANY],
         out_specs=[ANY, ANY],
         scratch_shapes=[
             pltpu.VMEM((B, HALF, LANES), F32),
@@ -294,7 +296,7 @@
         ],
         cost_estimate=pl.CostEstimate(flops=300 * B**3, transcendentals=0, bytes_accessed=40 * B**3),
         name="pairs",
-    )(scalars, lane_mixers(), boxes, peers)
+    )(partners, offsets, lane_mixers(), boxes, peers)
 
 
 def from_behind(array, axis, by):
@@ -309,24 +311,19 @@
 
 def local(orbitals, previous, potential, partners, offsets):
     slabs = lax.axis_size("grid")
-    total = lax.axis_size("orb") * slabs
     index = lax.axis_index("grid")
     core = index & 1
-    place = lax.axis_index(("orb", "grid"))
-    dist = jnp.remainder(partners[0] - place, total)
-    scalars = jnp.concatenate([core[None], dist, offsets.reshape(-1)])
     slab = jnp.stack([index, jnp.int32(slabs)])
 
     upper = from_behind(orbitals[:AHEAD], "orb", -1)
     longer = jnp.concatenate([orbitals, upper], axis=0)
     windows = jnp.stack([longer[:slabs], longer[2 : 2 + slabs], longer[4 : 4 + slabs]], axis=1)
-    windows, scalars = lax.optimization_barrier((windows, scalars))
     boxes = lax.all_to_all(windows, "grid", split_axis=0, concat_axis=0, tiled=True)
     peers = core_swap(boxes)
     source, _ = lax.optimization_barrier((orbitals, boxes))
     low = from_behind(source, "grid", 2)
     high = from_behind(source, "grid", -2)
-    kept, sent = pair_forces(scalars, boxes, peers)
+    kept, sent = pair_forces(partners, offsets, boxes, peers)
     given = core_swap(sent)
     summed = lax.dynamic_update_slice_in_dim(
         kept, lax.dynamic_slice_in_dim(kept, 1 - core, 2, axis=1) + given, 1 - core, axis=1

time: 244 us -> 243 us (level)
  transfers between devices with their start and end apart: 10 -> 10, of which waited for: 6 -> 6; matrix products, arithmetic and copies ran while one was open for 2% -> 1% of each run, Pallas kernels for 3% -> 3%
where the time goes in v6:
time: 243 us
  waiting for transfers between devices  105 us (43%)
  blocking collectives  86 us (35%)
  Pallas kernels  21.5 us (9%)
  starting transfers between devices  18.3 us (8%)
  other arithmetic  6.45 us (3%)
  local copies, waits for them, and re-layouts  4.95 us (2%)
    ppermute x4, waiting for transfers between devices, from_behind(): lax.ppermute(array, axis, [(i, (i + by) % count) for i in range(count)])  94 us
    all_to_all x1, blocking collectives, local(): lax.all_to_all(windows, 'grid', split_axis=0, concat_axis=0, tiled=True)  86 us
    pallas_call x1, Pallas kernels, pair_forces(): pl.pallas_call(pairs_kernel, out_shape=[jax.ShapeDtypeStruct((B, 3, HALF,...  13.7 us
    ppermute x5, waiting for transfers between devices, core_swap(): return lax.ppermute(array, 'grid', [(i, i ^ 1) for i in range(count)])  11 us
    ppermute x4, starting transfers between devices, from_behind(): lax.ppermute(array, axis, [(i, (i + by) % count) for i in range(count)])  9.52 us
    pallas_call x1, Pallas kernels, slab_terms(): pl.pallas_call(slab_kernel, grid=(arrays[0].shape[0] // GROUP,), out_shap...  7.72 us
    all_to_all x1, starting transfers between devices, local(): lax.all_to_all(summed, 'grid', split_axis=0, concat_axis=0, tiled=True)  5.37 us
  transfers between devices with their start and end apart: 10, of which 6 were waited for; matrix products, arithmetic and copies ran while one was open for 1% of the time, Pallas kernels for 3%

profile of v6, /device:TPU:1, one launch (start us, length us, event | category | flops | bytes accessed | tf_op | source)
XLA Modules:
  0.0 242.8 jit_solution(15460151761870936682)
XLA Ops:
  0.6 0.8 slice.51
  1.5 3.6 %collective-permute-start = (f32[4,32,128]{2,1,0:T(8,128)S(1)}, f32[4,32,128]{2,1,0:T(8,128)S(1)}, u32[]{:S(2)}, u32[]{:S(2)}) collective-permute-start(f32[4,32,128]{2,1,0:T(8,128)S(1)} %slice.51), channel_id=1, source_target_pairs={{0,192},{64,0},{128,64},{192,128},{1,193},{65,1},{129,65},{193,129... | collective-permute-start | bytes 196616 | tf_op jit(solution)/shard_map/ppermute | solution.py:304
  5.0 1.3 constant_dynamic-update-slice_fusion.1
  6.3 0.0 collective-permute-done
  6.4 0.2 slice_bitcast_fusion.2
  6.6 0.4 pad_maximum_fusion
  7.0 0.0 copy-start.7
  7.1 86.0 %all_to_all.10.boxes = f32[64,3,32,128]{3,2,1,0:T(8,128)S(1)} all-to-all(f32[64,3,32,128]{3,2,1,0:T(8,128)S(1)} %pad_maximum_fusion), channel_id=1, replica_groups=mesh['orb'=4,'grid'=64] {'grid'}, dimensions={0} | all-to-all | bytes 6291456 | tf_op jit(solution)/shard_map/all_to_all | solution.py:321
  93.0 1.1 collective-permute-start.6
  94.1 0.6 copy.10.offsets
  94.7 4.8 %collective-permute-done.6.peers = f32[64,3,32,128]{3,2,1,0:T(8,128)} collective-permute-done((f32[64,3,32,128]{3,2,1,0:T(8,128)S(1)}, f32[64,3,32,128]{3,2,1,0:T(8,128)}, u32[]{:S(2)}, u32[]{:S(2)}) %collective-permute-start.6) | collective-permute-done | bytes 3145760 | tf_op jit(solution)/shard_map/ppermute | solution.py:309
  99.5 13.7 %pairs.1 = (f32[64,3,32,128]{3,2,1,0:T(8,128)}, f32[64,2,32,128]{3,2,1,0:T(8,128)}) custom-call(s32[1,3]{1,0:T(1,128)} %partners.1, s32[1,3,3]{2,1,0:T(4,128)} %copy.10.offsets, bf16[512,128]{1,0:T(8,128)(2,1)} %constant.19.clone.mix, f32[64,3,32,128]{3,2,1,0:T(8,128)} %copy-done, f32[64,3,32,128]{3,2,1,0:T(8,128)} %collective-permute-done.6.peers), custom_call_target="tpu_custom_call" | custom-call | flops 78643200 | bytes 10485760 | tf_op jit(solution)/shard_map/pairs/pallas_call | solution.py:278
  113.3 0.5 collective-permute-start.7
  113.8 4.0 %collective-permute-done.7 = f32[64,2,32,128]{3,2,1,0:T(8,128)S(1)} collective-permute-done((f32[64,2,32,128]{3,2,1,0:T(8,128)}, f32[64,2,32,128]{3,2,1,0:T(8,128)S(1)}, u32[]{:S(2)}, u32[]{:S(2)}) %collective-permute-start.7) | collective-permute-done | bytes 2097184 | tf_op jit(solution)/shard_map/ppermute | solution.py:309
  117.8 3.5 %add_dynamic-update-slice_fusion = f32[64,3,32,128]{3,2,1,0:T(8,128)} fusion(f32[64,3,32,128]{3,2,1,0:T(8,128)} %get-tuple-element.6, s32[]{:T(128)S(6)} %select_n.4, f32[64,2,32,128]{3,2,1,0:T(8,128)S(1)} %collective-permute-done.7), kind=kLoop, calls=%fused_computation.1 | loop fusion | flops 524288 | bytes 6291460 | tf_op jit(solution)/shard_map/dynamic_update_slice | solution.py:328
  121.3 5.4 %all-to-all-start.1 = ((f32[64,3,32,128]{3,2,1,0:T(8,128)}), f32[64,3,32,128]{3,2,1,0:T(8,128)S(1)}, u32[]{:S(2)}, u32[]{:S(2)}) async-start(f32[64,3,32,128]{3,2,1,0:T(8,128)} %add_dynamic-update-slice_fusion), calls=%async_computation.1 | async-start | bytes 6291456 | tf_op jit(solution)/shard_map/all_to_all | solution.py:331
  126.6 1.4 collective-permute-start.1
  128.1 3.7 %collective-permute-start.2 = (f32[64,32,128]{2,1,0:T(8,128)}, f32[64,32,128]{2,1,0:T(8,128)S(1)}, u32[]{:S(2)}, u32[]{:S(2)}) collective-permute-start(f32[64,32,128]{2,1,0:T(8,128)} %own.1), channel_id=1, source_target_pairs={{0,62},{1,63},{2,0},{3,1},{4,2},{5,3},{6,4},{7,5},{8,6},{9,7},{10,... | collective-permute-start | bytes 3145736 | tf_op jit(solution)/shard_map/ppermute | solution.py:304
  131.8 0.7 collective-permute-start.3
  132.5 89.5 %collective-permute-done.1.low = f32[64,32,128]{2,1,0:T(8,128)S(1)} collective-permute-done((f32[64,32,128]{2,1,0:T(8,128)}, f32[64,32,128]{2,1,0:T(8,128)S(1)}, u32[]{:S(2)}, u32[]{:S(2)}) %collective-permute-start.1) | collective-permute-done | bytes 1048608 | tf_op jit(solution)/shard_map/ppermute | solution.py:304
  222.0 1.0 copy-done.3
  223.0 1.0 collective-permute-start.4
  224.0 0.1 collective-permute-start.5
  224.1 0.7 pad_add_fusion.place
  224.8 1.5 collective-permute-done.4.peer_low
  226.2 1.0 copy-done.6
  227.2 0.6 collective-permute-done.5.peer_high
  227.9 7.7 %slab.1 = f32[64,32,128]{2,1,0:T(8,128)} custom-call(s32[2]{0:T(128)} %pad_add_fusion.place, bf16[512,128]{1,0:T(8,128)(2,1)} %constant.19.clone.mix, f32[64,32,128]{2,1,0:T(8,128)} %own.1, f32[64,32,128]{2,1,0:T(8,128)} %copy-done.3, f32[64,32,128]{2,1,0:T(8,128)} %copy-done.4, f32[64,32,128]{2,1,0:T(8,128)} %copy-done.5, f32[64,32,128]{2,1,0:T(8,128)} %copy-done.6, ...), custom_call_target="tpu_custom_call" | custom-call | flops 5242880 | bytes 9437184 | tf_op jit(solution)/shard_map/slab/pallas_call | solution.py:264
  235.6 0.8 collective-permute-start.8
  236.5 0.2 fusion.1
  236.7 4.5 %collective-permute-done.8 = f32[4,32,128]{2,1,0:T(8,128)S(1)} collective-permute-done((f32[4,32,128]{2,1,0:T(8,128)S(1)}, f32[4,32,128]{2,1,0:T(8,128)S(1)}, u32[]{:S(2)}, u32[]{:S(2)}) %collective-permute-start.8) | collective-permute-done | bytes 65568 | tf_op jit(solution)/shard_map/ppermute | solution.py:304
  241.2 1.7 multiply_add_fusion
  (20 shorter events, 0.1 us)
Async XLA Ops:
  1.5 5.2 %copy-start.1 = (f32[64,32,128]{2,1,0:T(8,128)S(1)}, f32[64,32,128]{2,1,0:T(8,128)}, u32[]{:S(2)}) copy-start(f32[64,32,128]{2,1,0:T(8,128)} %own.1) | copy-start | bytes 3145732
  1.5 4.9 %collective-permute-start = (f32[4,32,128]{2,1,0:T(8,128)S(1)}, f32[4,32,128]{2,1,0:T(8,128)S(1)}, u32[]{:S(2)}, u32[]{:S(2)}) collective-permute-start(f32[4,32,128]{2,1,0:T(8,128)S(1)} %slice.51), channel_id=1, source_target_pairs={{0,192},{64,0},{128,64},{192,128},{1,193},{65,1},{129,65},{193,129... | collective-permute-start | bytes 196616 | tf_op jit(solution)/shard_map/ppermute | solution.py:304
  7.0 87.1 %copy-start.7 = (s32[1,3,3]{2,0,1:T(1,128)S(1)}, s32[1,3,3]{2,0,1:T(1,128)}, u32[]{:S(2)}) copy-start(s32[1,3,3]{2,0,1:T(1,128)} %param.11) | copy-start | bytes 112
  93.0 6.5 %copy-start = (f32[64,3,32,128]{3,2,1,0:T(8,128)}, f32[64,3,32,128]{3,2,1,0:T(8,128)S(1)}, u32[]{:S(2)}) copy-start(f32[64,3,32,128]{3,2,1,0:T(8,128)S(1)} %all_to_all.10.boxes) | copy-start | bytes 9437188
  93.0 6.5 %collective-permute-start.6 = (f32[64,3,32,128]{3,2,1,0:T(8,128)S(1)}, f32[64,3,32,128]{3,2,1,0:T(8,128)}, u32[]{:S(2)}, u32[]{:S(2)}) collective-permute-start(f32[64,3,32,128]{3,2,1,0:T(8,128)S(1)} %all_to_all.10.boxes), channel_id=1, source_target_pairs={{0,1},{1,0},{2,3},{3,2},{4,5},{5,4},{6,7},{7,6},{8,9},{9,8},{10,11... | collective-permute-start | bytes 9437192 | tf_op jit(solution)/shard_map/ppermute | solution.py:309
  113.3 4.5 %collective-permute-start.7 = (f32[64,2,32,128]{3,2,1,0:T(8,128)}, f32[64,2,32,128]{3,2,1,0:T(8,128)S(1)}, u32[]{:S(2)}, u32[]{:S(2)}) collective-permute-start(f32[64,2,32,128]{3,2,1,0:T(8,128)} %get-tuple-element.7), channel_id=1, source_target_pairs={{0,1},{1,0},{2,3},{3,2},{4,5},{5,4},{6,7},{7,6},{8,9},{9,8},{10,11... | collective-permute-start | bytes 6291464 | tf_op jit(solution)/shard_map/ppermute | solution.py:309
  121.3 114.3 %all-to-all-start.1 = ((f32[64,3,32,128]{3,2,1,0:T(8,128)}), f32[64,3,32,128]{3,2,1,0:T(8,128)S(1)}, u32[]{:S(2)}, u32[]{:S(2)}) async-start(f32[64,3,32,128]{3,2,1,0:T(8,128)} %add_dynamic-update-slice_fusion), calls=%async_computation.1 | async-start | bytes 6291456 | tf_op jit(solution)/shard_map/all_to_all | solution.py:331
  126.6 95.4 %collective-permute-start.1 = (f32[64,32,128]{2,1,0:T(8,128)}, f32[64,32,128]{2,1,0:T(8,128)S(1)}, u32[]{:S(2)}, u32[]{:S(2)}) collective-permute-start(f32[64,32,128]{2,1,0:T(8,128)} %own.1), channel_id=1, source_target_pairs={{0,2},{1,3},{2,4},{3,5},{4,6},{5,7},{6,8},{7,9},{8,10},{9,11},{10,... | collective-permute-start | bytes 3145736 | tf_op jit(solution)/shard_map/ppermute | solution.py:304
  128.1 95.9 %collective-permute-start.2 = (f32[64,32,128]{2,1,0:T(8,128)}, f32[64,32,128]{2,1,0:T(8,128)S(1)}, u32[]{:S(2)}, u32[]{:S(2)}) collective-permute-start(f32[64,32,128]{2,1,0:T(8,128)} %own.1), channel_id=1, source_target_pairs={{0,62},{1,63},{2,0},{3,1},{4,2},{5,3},{6,4},{7,5},{8,6},{9,7},{10,... | collective-permute-start | bytes 3145736 | tf_op jit(solution)/shard_map/ppermute | solution.py:304
  131.8 93.0 %collective-permute-start.3 = (f32[64,32,128]{2,1,0:T(8,128)}, f32[64,32,128]{2,1,0:T(8,128)S(1)}, u32[]{:S(2)}, u32[]{:S(2)}) collective-permute-start(f32[64,32,128]{2,1,0:T(8,128)} %own.1), channel_id=1, source_target_pairs={{0,1},{1,0},{2,3},{3,2},{4,5},{5,4},{6,7},{7,6},{8,9},{9,8},{10,11... | collective-permute-start | bytes 3145736 | tf_op jit(solution)/shard_map/ppermute | solution.py:309
  222.0 1.0 copy-start.3
  223.0 3.3 %collective-permute-start.4 = (f32[64,32,128]{2,1,0:T(8,128)S(1)}, f32[64,32,128]{2,1,0:T(8,128)S(1)}, u32[]{:S(2)}, u32[]{:S(2)}) collective-permute-start(f32[64,32,128]{2,1,0:T(8,128)S(1)} %collective-permute-done.1.low), channel_id=1, source_target_pairs={{0,1},{1,0},{2,3},{3,2},{4,5},{5,4},{6,7},{7,6},{8,9},{9,8},{10,11... | collective-permute-start | bytes 3145736 | tf_op jit(solution)/shard_map/ppermute | solution.py:309
  224.0 2.3 copy-start.4
  224.0 3.9 %collective-permute-start.5 = (f32[64,32,128]{2,1,0:T(8,128)S(1)}, f32[64,32,128]{2,1,0:T(8,128)}, u32[]{:S(2)}, u32[]{:S(2)}) collective-permute-start(f32[64,32,128]{2,1,0:T(8,128)S(1)} %collective-permute-done.2.high), channel_id=1, source_target_pairs={{0,1},{1,0},{2,3},{3,2},{4,5},{5,4},{6,7},{7,6},{8,9},{9,8},{10,11... | collective-permute-start | bytes 3145736 | tf_op jit(solution)/shard_map/ppermute | solution.py:309
  224.8 1.5 copy-start.5
  226.2 1.0 copy-start.6
  235.6 5.6 %copy-start.2 = (f32[64,32,128]{2,1,0:T(8,128)S(1)}, f32[64,32,128]{2,1,0:T(8,128)}, u32[]{:S(2)}) copy-start(f32[64,32,128]{2,1,0:T(8,128)} %slab.1) | copy-start | bytes 3145732
  235.6 5.5 %collective-permute-start.8 = (f32[4,32,128]{2,1,0:T(8,128)S(1)}, f32[4,32,128]{2,1,0:T(8,128)S(1)}, u32[]{:S(2)}, u32[]{:S(2)}) collective-permute-start(f32[4,32,128]{2,1,0:T(8,128)S(1)} %fusion.2), channel_id=1, source_target_pairs={{0,64},{64,128},{128,192},{192,0},{1,65},{65,129},{129,193},{193,1... | collective-permute-start | bytes 196616 | tf_op jit(solution)/shard_map/ppermute | solution.py:304
